TPU v7x, 8 devices: a whole 2x2x1 slice. The times are simulated.
8 devices in a mesh: col: 2 (over z, y), row: 4 (over x, core).
Axes of the slice: x: 2, y: 2, z: 1, core: 2. Of those that a mesh axis runs over, the one named last changes fastest.
Arguments:
- inter_mask: int32 [8192, 16384], P('row', 'col')
- user_emb: bfloat16 [8192, 64], P(('row', 'col'))
- item_emb: bfloat16 [16384, 64], P(('col', 'row'))
- triples: int32 [8192, 3], replicated
Outputs:
- output 1: bfloat16 [8192, 64], P(('row', 'col'))
- output 2: bfloat16 [16384, 64], P(('col', 'row'))
- output 3: float32 [], replicated
- output 4: float32 [8192, 64], P(('row', 'col'))
- output 5: float32 [16384, 64], P(('col', 'row'))
All inputs are finite; a program needn't handle non-finite values.
Results may differ from a plain program's by a relative error of at most 0.0104521.
Values are sent between devices in bfloat16 or wider.
A program may use at most 1 GiB of HBM per device.

v0:
```python
import jax
import jax.numpy as jnp
from jax import lax
from jax.sharding import PartitionSpec as P, NamedSharding

LAYERS = 3


def solution(mesh):
    n_col = mesh.shape['col']
    n_row = mesh.shape['row']

    def local_fn(mask_blk, user_emb, item_emb, triples):
        row_idx = lax.axis_index('row')
        col_idx = lax.axis_index('col')
        user_rows = user_emb.shape[0]
        item_rows = item_emb.shape[0]
        n_batch = triples.shape[0]

        deg_user = jnp.maximum(lax.psum(jnp.sum(mask_blk, axis=1, dtype=jnp.int32), 'col'), 1)
        deg_item = jnp.maximum(lax.psum(jnp.sum(mask_blk, axis=0, dtype=jnp.int32), 'row'), 1)
        scale_user = lax.rsqrt(deg_user.astype(jnp.float32))
        scale_item = lax.rsqrt(deg_item.astype(jnp.float32))
        adj_blk = (scale_user[:, None] * mask_blk.astype(jnp.float32) * scale_item[None, :]).astype(jnp.bfloat16)

        def user_half(item_shard):
            gathered = lax.all_gather(item_shard, 'row', axis=0, tiled=True)
            partial_sum = jnp.dot(adj_blk, gathered, preferred_element_type=jnp.float32)
            return lax.psum_scatter(partial_sum, 'col', scatter_dimension=0, tiled=True)

        def item_half(user_shard):
            gathered = lax.all_gather(user_shard, 'col', axis=0, tiled=True)
            partial_sum = lax.dot_general(adj_blk, gathered, (((0,), (0,)), ((), ())), preferred_element_type=jnp.float32)
            return lax.psum_scatter(partial_sum, 'row', scatter_dimension=0, tiled=True)

        user_cur = user_emb
        item_cur = item_emb
        user_acc = user_emb.astype(jnp.float32)
        item_acc = item_emb.astype(jnp.float32)
        for _ in range(LAYERS):
            user_next = user_half(item_cur).astype(jnp.bfloat16)
            item_next = item_half(user_cur).astype(jnp.bfloat16)
            user_acc = user_acc + user_next.astype(jnp.float32)
            item_acc = item_acc + item_next.astype(jnp.float32)
            user_cur, item_cur = user_next, item_next
        user_final = (user_acc / (LAYERS + 1)).astype(jnp.bfloat16)
        item_final = (item_acc / (LAYERS + 1)).astype(jnp.bfloat16)

        user_base = (row_idx * n_col + col_idx) * user_rows
        item_base = (col_idx * n_row + row_idx) * item_rows
        local_user = triples[:, 0] - user_base
        local_pos = triples[:, 1] - item_base
        local_neg = triples[:, 2] - item_base

        def lookup_rows(emb_table, local_ids):
            is_owned = (local_ids >= 0) & (local_ids < emb_table.shape[0])
            picked = jnp.take(emb_table, jnp.clip(local_ids, 0, emb_table.shape[0] - 1), axis=0).astype(jnp.float32)
            seg_ids = jnp.where(is_owned, local_ids, emb_table.shape[0])
            return jnp.where(is_owned[:, None], picked, 0.0), seg_ids

        rows_user, seg_user = lookup_rows(user_final, local_user)
        rows_pos, seg_pos = lookup_rows(item_final, local_pos)
        rows_neg, seg_neg = lookup_rows(item_final, local_neg)
        fetched = lax.psum(jnp.concatenate([rows_user, rows_pos, rows_neg], axis=0), ('row', 'col'))
        e_user = fetched[:n_batch]
        e_pos = fetched[n_batch:2 * n_batch]
        e_neg = fetched[2 * n_batch:]
        margin = jnp.sum(e_user * e_pos, axis=1) - jnp.sum(e_user * e_neg, axis=1)
        bpr_loss = jnp.mean(jax.nn.softplus(-margin))
        loss_coef = -jax.nn.sigmoid(-margin) / n_batch
        grad_eu = loss_coef[:, None] * (e_pos - e_neg)
        grad_epos = loss_coef[:, None] * e_user
        seed_user = jax.ops.segment_sum(grad_eu, seg_user, num_segments=user_rows)
        seed_item = jax.ops.segment_sum(jnp.concatenate([grad_epos, -grad_epos], axis=0), jnp.concatenate([seg_pos, seg_neg], axis=0), num_segments=item_rows)

        src_user = seed_user / (LAYERS + 1)
        src_item = seed_item / (LAYERS + 1)
        cot_user = src_user.astype(jnp.bfloat16)
        cot_item = src_item.astype(jnp.bfloat16)
        for _ in range(LAYERS - 1):
            new_user = (src_user + user_half(cot_item)).astype(jnp.bfloat16)
            new_item = (src_item + item_half(cot_user)).astype(jnp.bfloat16)
            cot_user, cot_item = new_user, new_item
        grad_user = src_user + user_half(cot_item)
        grad_item = src_item + item_half(cot_user)
        return user_final, item_final, bpr_loss, grad_user, grad_item

    user_spec = P(('row', 'col'), None)
    item_spec = P(('col', 'row'), None)
    return jax.shard_map(local_fn, mesh=mesh, in_specs=(P('row', 'col'), user_spec, item_spec, P()), out_specs=(user_spec, item_spec, P(), user_spec, item_spec), check_vma=False)
```

profile of v0, /device:TPU:0, one launch (start us, length us, event | category | flops | bytes accessed | tf_op | source)
XLA Modules:
  0.0 917.3 jit_solution(12063033747222443853)
XLA Ops:
  7.2 0.7 all-gather.7.cloned.1.call-update
  8.0 20.8 %fusion.16 = (s32[2048]{0:T(1024)S(1)}, s32[8192]{0:T(1024)S(1)}) fusion(s32[2048,8192]{1,0:T(8,128)} %param.6), kind=kLoop, calls=%fused_computation.60 | loop fusion | flops 33544192 | bytes 67149824 | tf_op jit(solution)/shard_map/reduce_sum | solution.py:20
  28.8 13.3 %psum.22 = s32[8192]{0:T(1024)S(1)} all-reduce(s32[8192]{0:T(1024)S(1)} %get-tuple-element.7), channel_id=1, replica_groups=mesh['col'=2,'row'=4] {'row'}, use_global_device_ids=true, to_apply=%region_3.0 | all-reduce | flops 8192 | bytes 65536 | tf_op jit(solution)/shard_map/psum | solution.py:21
  42.1 4.3 psum.21
  46.5 5.6 all_gather.37
  52.1 32.7 %multiply_convert_fusion = bf16[2048,8192]{1,0:T(8,128)(2,1)} fusion(s32[2048,8192]{1,0:T(8,128)} %param.6, f32[8192]{0:T(1024)S(1)} %convert_rsqrt_fusion, f32[2048]{0:T(1024)S(1)} %convert_rsqrt_fusion.1), kind=kLoop, calls=%fused_computation.5 | loop fusion | flops 67108864 | bytes 100704256 | tf_op jit(solution)/shard_map/convert_element_type | solution.py:24
  84.8 14.9 %fusion.24 = f32[8192,64]{0,1:T(8,128)} fusion(bf16[2048,64]{0,1:T(8,128)(2,1)S(1)} %all_gather.37, bf16[2048,8192]{1,0:T(8,128)(2,1)} %multiply_convert_fusion), kind=kOutput, calls=%fused_computation.68 | convolution fusion | flops 2147483648 | bytes 35913728 | tf_op jit(solution)/shard_map/dot_general | solution.py:33
  99.8 21.8 %fusion.18 = f32[2048,64]{0,1:T(8,128)} fusion(bf16[2048,8192]{1,0:T(8,128)(2,1)} %multiply_convert_fusion, bf16[8192,64]{0,1:T(8,128)(2,1)} %all-gather.7.cloned.1.call-done), kind=kOutput, calls=%fused_computation.62 | convolution fusion | flops 2147483648 | bytes 35127296 | tf_op jit(solution)/shard_map/dot_general | solution.py:28
  121.7 3.8 reduce-scatter.15.cloned.1.call-done
  125.4 1.8 convert_element_type.94
  127.3 12.7 %reduce-scatter.13.cloned.1.call-done = f32[1024,64]{0,1:T(8,128)} async-done(((f32[2048,64]{0,1:T(8,128)}), f32[1024,64]{0,1:T(8,128)}) %reduce-scatter.13.cloned.1.call-update) | async-done | bytes 262160 | tf_op jit(solution)/shard_map/reduce_scatter | solution.py:29
  140.0 1.0 convert_element_type.92
  141.0 5.8 all_gather.39
  146.8 8.9 all-gather.9.cloned.1.call-done
  155.7 21.9 %fusion.19 = f32[2048,64]{0,1:T(8,128)} fusion(bf16[2048,8192]{1,0:T(8,128)(2,1)} %multiply_convert_fusion, bf16[8192,64]{0,1:T(8,128)(2,1)} %all-gather.9.cloned.1.call-done), kind=kOutput, calls=%fused_computation.63 | convolution fusion | flops 2147483648 | bytes 35127296 | tf_op jit(solution)/shard_map/dot_general | solution.py:28
  177.7 14.9 %fusion.25 = f32[8192,64]{0,1:T(8,128)} fusion(bf16[2048,64]{0,1:T(8,128)(2,1)S(1)} %all_gather.39, bf16[2048,8192]{1,0:T(8,128)(2,1)} %multiply_convert_fusion), kind=kOutput, calls=%fused_computation.69 | convolution fusion | flops 2147483648 | bytes 35913728 | tf_op jit(solution)/shard_map/dot_general | solution.py:33
  192.6 1.0 convert_element_type.95
  193.6 6.3 all_gather.41
  199.9 15.0 %fusion.26 = f32[8192,64]{0,1:T(8,128)} fusion(bf16[2048,64]{0,1:T(8,128)(2,1)S(1)} %all_gather.41, bf16[2048,8192]{1,0:T(8,128)(2,1)} %multiply_convert_fusion), kind=kOutput, calls=%fused_computation.70 | convolution fusion | flops 2147483648 | bytes 35913728 | tf_op jit(solution)/shard_map/dot_general | solution.py:33
  214.9 0.3 all-gather.11.cloned.1.call-start
  215.2 3.1 reduce-scatter.19.cloned.1.call-done
  218.2 28.0 %reduce-scatter.23.cloned.1.call-done = f32[2048,64]{0,1:T(8,128)} async-done(((f32[8192,64]{0,1:T(8,128)}), f32[2048,64]{0,1:T(8,128)}) %reduce-scatter.23.cloned.1.call-update) | async-done | bytes 524304 | tf_op jit(solution)/shard_map/reduce_scatter | solution.py:34
  246.3 2.0 multiply_convert_fusion.1
  248.4 0.5 and_reduce_fusion.2
  249.1 0.3 copy.16
  249.4 24.0 %gather_fusion.1 = bf16[8192,64]{1,0:T(8,128)(2,1)S(1)} fusion(bf16[2048,64]{1,0:T(8,128)(2,1)S(1)} %copy.16, s32[8192]{0:T(1024)S(1)} %get-tuple-element.35), kind=kCustom, calls=%fused_computation.clone | custom fusion | bytes 2129920 | tf_op jit(solution)/shard_map/jit(_take)/gather | solution.py:57
  273.4 29.4 %gather_fusion.2 = bf16[8192,64]{1,0:T(8,128)(2,1)} fusion(bf16[2048,64]{1,0:T(8,128)(2,1)S(1)} %copy.16, s32[8192]{0:T(1024)S(1)} %get-tuple-element.37), kind=kCustom, calls=%fused_computation.1.clone | custom fusion | bytes 2129920 | tf_op jit(solution)/shard_map/jit(_take)/gather | solution.py:57
  302.8 21.9 %fusion.20 = f32[2048,64]{0,1:T(8,128)} fusion(bf16[2048,8192]{1,0:T(8,128)(2,1)} %multiply_convert_fusion, bf16[8192,64]{0,1:T(8,128)(2,1)} %all-gather.11.cloned.1.call-done), kind=kOutput, calls=%fused_computation.64 | convolution fusion | flops 2147483648 | bytes 35127296 | tf_op jit(solution)/shard_map/dot_general | solution.py:28
  324.7 0.4 all-reduce.2.cloned.1.call-start
  325.2 9.2 %convert_select_fusion = (f32[8192,64]{1,0:T(8,128)}, f32[8192,64]{1,0:T(8,128)}) fusion(bf16[8192,64]{1,0:T(8,128)(2,1)} %gather_fusion.2, pred[8192]{0:T(1024)(128)(4,1)S(1)} %compare_and_fusion.1, pred[8192]{0:T(1024)(128)(4,1)S(1)} %get-tuple-element.28, bf16[8192,64]{1,0:T(8,128)(2,1)S(1)} %gather_fusion.1, pred[8192]{0:T(1024)(128)(4,1)S(1)} %compare_and_fusion.2, ...), kind=kLoop, calls=%fused_computation.16 | loop fusion | flops 3145728 | bytes 6324224 | tf_op jit(solution)/shard_map/jit(_where)/select_n | solution.py:59
  334.4 2.2 reduce-scatter.21.cloned.1.call-done
  336.6 1.0 multiply_convert_fusion.3
  337.8 24.0 %gather_fusion = bf16[8192,64]{1,0:T(8,128)(2,1)S(1)} fusion(bf16[1024,64]{1,0:T(8,128)(2,1)S(1)} %copy.15, s32[8192]{0:T(1024)S(1)} %broadcast_clamp_fusion), kind=kCustom, calls=%fused_computation.2 | custom fusion | bytes 2129920 | tf_op jit(solution)/shard_map/jit(_take)/gather | solution.py:57
  361.9 2.5 convert_select_fusion.2
  364.4 11.8 %pad_maximum_fusion = f32[24576,64]{1,0:T(8,128)} fusion(f32[8192,64]{1,0:T(8,128)S(1)} %copy-done, f32[8192,64]{1,0:T(8,128)} %get-tuple-element.39, f32[8192,64]{1,0:T(8,128)S(1)} %convert_select_fusion.2), kind=kLoop, calls=%fused_computation.6 | loop fusion | flops 3145728 | bytes 12582912 | tf_op jit(solution)/shard_map/concatenate | solution.py:64
  376.3 160.4 %all-reduce.2.cloned.1.call-done = f32[24576,64]{1,0:T(8,128)} async-done(((f32[24576,64]{1,0:T(8,128)}), f32[24576,64]{1,0:T(8,128)}) %all-reduce.2.cloned.1.call-update) | async-done | bytes 6291472 | tf_op jit(solution)/shard_map/psum | solution.py:64
  536.7 6.9 multiply_reduce_fusion
  543.6 0.6 negate_multiply_fusion
  544.2 48.8 %scatter_custom_fusion = f32[1024,64]{1,0:T(8,128)S(1)} fusion(s32[8192]{0:T(1024)S(1)} %bitcast.33, f32[24576,64]{1,0:T(8,128)} %all-reduce.2.cloned.1.call-done, f32[8192]{0:T(1024)S(1)} %get-tuple-element.32, f32[]{:T(128)} %constant.36.clone.1), kind=kCustom, calls=%fused_computation.11 | custom fusion | flops 1572864 | bytes 8684032 | tf_op jit(solution)/shard_map/scatter-add | solution.py:73
  593.2 5.6 all_gather.45
  598.8 14.9 %fusion.28 = f32[8192,64]{0,1:T(8,128)} fusion(bf16[2048,64]{0,1:T(8,128)(2,1)S(1)} %all_gather.45, bf16[2048,8192]{1,0:T(8,128)(2,1)} %multiply_convert_fusion), kind=kOutput, calls=%fused_computation.72 | convolution fusion | flops 2147483648 | bytes 35913728 | tf_op jit(solution)/shard_map/dot_general | solution.py:33
  614.0 5.4 fusion.17
  619.4 90.7 %scatter_custom_fusion.1 = f32[2048,64]{1,0:T(8,128)S(1)} fusion(s32[16384]{0:T(1024)S(1)} %pad_add_fusion, f32[8192,64]{1,0:T(8,128)} %get-tuple-element.10, f32[]{:T(128)} %constant.76, f32[8192,64]{1,0:T(8,128)} %get-tuple-element.11, f32[]{:T(128)} %constant.36.clone.1), kind=kCustom, calls=%fused_computation.7 | custom fusion | flops 2097152 | bytes 4718600 | tf_op jit(solution)/shard_map/scatter-add | solution.py:74
  710.1 0.3 copy.19
  710.5 1.9 add_convert_fusion
  712.4 0.7 all-gather.17.cloned.1.call-update
  713.2 13.3 %all-gather.13.cloned.1.call-done = bf16[8192,64]{0,1:T(8,128)(2,1)} async-done(((bf16[2048,64]{0,1:T(8,128)(2,1)}), bf16[8192,64]{0,1:T(8,128)(2,1)}) %all-gather.13.cloned.1.call-update) | async-done | bytes 1048592 | tf_op jit(solution)/shard_map/all_gather | solution.py:27
  726.5 21.9 %fusion.21 = f32[2048,64]{0,1:T(8,128)} fusion(bf16[2048,8192]{1,0:T(8,128)(2,1)} %multiply_convert_fusion, bf16[8192,64]{0,1:T(8,128)(2,1)} %all-gather.13.cloned.1.call-done), kind=kOutput, calls=%fused_computation.65 | convolution fusion | flops 2147483648 | bytes 35127296 | tf_op jit(solution)/shard_map/dot_general | solution.py:28
  748.4 0.3 reduce-scatter.33.cloned.1.call-start
  748.7 21.9 %fusion.23 = f32[2048,64]{0,1:T(8,128)} fusion(bf16[2048,8192]{1,0:T(8,128)(2,1)} %multiply_convert_fusion, bf16[8192,64]{0,1:T(8,128)(2,1)} %all-gather.17.cloned.1.call-done), kind=kOutput, calls=%fused_computation.67 | convolution fusion | flops 2147483648 | bytes 35127296 | tf_op jit(solution)/shard_map/dot_general | solution.py:28
  770.6 11.8 %reduce-scatter.33.cloned.1.call-done = f32[1024,64]{0,1:T(8,128)} async-done(((f32[2048,64]{0,1:T(8,128)}), f32[1024,64]{0,1:T(8,128)}) %reduce-scatter.33.cloned.1.call-update) | async-done | bytes 262160 | tf_op jit(solution)/shard_map/reduce_scatter | solution.py:29
  782.5 1.1 add_convert_fusion.2
  783.5 5.7 all_gather.43
  789.2 14.9 %fusion.27 = f32[8192,64]{0,1:T(8,128)} fusion(bf16[2048,64]{0,1:T(8,128)(2,1)S(1)} %all_gather.43, bf16[2048,8192]{1,0:T(8,128)(2,1)} %multiply_convert_fusion), kind=kOutput, calls=%fused_computation.71 | convolution fusion | flops 2147483648 | bytes 35913728 | tf_op jit(solution)/shard_map/dot_general | solution.py:33
  804.1 5.6 all_gather.47
  809.8 14.9 %fusion.29 = f32[8192,64]{0,1:T(8,128)} fusion(bf16[2048,64]{0,1:T(8,128)(2,1)S(1)} %all_gather.47, bf16[2048,8192]{1,0:T(8,128)(2,1)} %multiply_convert_fusion), kind=kOutput, calls=%fused_computation.73 | convolution fusion | flops 2147483648 | bytes 35913728 | tf_op jit(solution)/shard_map/dot_general | solution.py:33
  824.7 0.3 all-gather.15.cloned.1.call-start
  825.0 4.7 reduce-scatter.27.cloned.1.call-done
  829.8 27.9 %reduce-scatter.35.cloned.1.call-done = f32[2048,64]{0,1:T(8,128)} async-done(((f32[8192,64]{0,1:T(8,128)}), f32[2048,64]{0,1:T(8,128)}) %reduce-scatter.35.cloned.1.call-update) | async-done | bytes 524304 | tf_op jit(solution)/shard_map/reduce_scatter | solution.py:34
  857.6 2.2 multiply_add_fusion
  859.9 13.8 %all-gather.15.cloned.1.call-done = bf16[8192,64]{0,1:T(8,128)(2,1)} async-done(((bf16[2048,64]{0,1:T(8,128)(2,1)}), bf16[8192,64]{0,1:T(8,128)(2,1)}) %all-gather.15.cloned.1.call-update) | async-done | bytes 1048592 | tf_op jit(solution)/shard_map/all_gather | solution.py:27
  873.7 21.9 %fusion.22 = f32[2048,64]{0,1:T(8,128)} fusion(bf16[2048,8192]{1,0:T(8,128)(2,1)} %multiply_convert_fusion, bf16[8192,64]{0,1:T(8,128)(2,1)} %all-gather.15.cloned.1.call-done), kind=kOutput, calls=%fused_computation.66 | convolution fusion | flops 2147483648 | bytes 35127296 | tf_op jit(solution)/shard_map/dot_general | solution.py:28
  896.2 11.3 %reduce-scatter.29.cloned.1.call-done = f32[1024,64]{0,1:T(8,128)} async-done(((f32[2048,64]{0,1:T(8,128)}), f32[1024,64]{0,1:T(8,128)}) %reduce-scatter.29.cloned.1.call-update) | async-done | bytes 262160 | tf_op jit(solution)/shard_map/reduce_scatter | solution.py:29
  907.5 1.7 multiply_add_fusion.1
  (68 shorter events, 1.7 us)
Async XLA Ops:
  7.2 92.6 %all-gather.7.cloned.1.call-start = ((), (), s32[]{:S(2)}) async-start(), calls=%async_computation.12 | async-start | bytes 1310720 | tf_op jit(solution)/shard_map/all_gather | solution.py:27
  7.9 38.6 %copy-start.6 = (bf16[1024,64]{0,1:T(8,128)(2,1)S(1)}, bf16[1024,64]{0,1:T(8,128)(2,1)}, u32[]{:S(2)}) copy-start(bf16[1024,64]{0,1:T(8,128)(2,1)} %param.7) | copy-start | bytes 393220
  7.9 117.5 %reduce-scatter.15.cloned.1.call-start = ((), (), s32[]{:S(2)}) async-start(), calls=%async_computation.14 | async-start | bytes 2621440 | tf_op jit(solution)/shard_map/reduce_scatter | solution.py:34
  99.7 40.3 %reduce-scatter.13.cloned.1.call-start = ((), (), s32[]{:S(2)}) async-start(), calls=%async_computation.13 | async-start | bytes 786432 | tf_op jit(solution)/shard_map/reduce_scatter | solution.py:29
  121.6 34.1 %all-gather.9.cloned.1.call-start = ((), (), s32[]{:S(2)}) async-start(), calls=%async_computation.15 | async-start | bytes 1310720 | tf_op jit(solution)/shard_map/all_gather | solution.py:27
  127.2 65.4 %reduce-scatter.17.cloned.1.call-start = ((), (), s32[]{:S(2)}) async-start(), calls=%async_computation.16 | async-start | bytes 786432 | tf_op jit(solution)/shard_map/reduce_scatter | solution.py:29
  177.6 40.6 %reduce-scatter.19.cloned.1.call-start = ((), (), s32[]{:S(2)}) async-start(), calls=%async_computation.17 | async-start | bytes 2621440 | tf_op jit(solution)/shard_map/reduce_scatter | solution.py:34
  192.6 53.7 %reduce-scatter.23.cloned.1.call-start = ((), (), s32[]{:S(2)}) async-start(), calls=%async_computation.20 | async-start | bytes 2621440 | tf_op jit(solution)/shard_map/reduce_scatter | solution.py:34
  199.9 46.4 %copy-start.1 = (f32[2048,64]{0,1:T(8,128)S(1)}, f32[2048,64]{0,1:T(8,128)}, u32[]{:S(2)}) copy-start(f32[2048,64]{0,1:T(8,128)} %reduce-scatter.15.cloned.1.call-done) | copy-start | bytes 1572868
  199.9 46.4 %copy-start.3 = (bf16[2048,64]{0,1:T(8,128)(2,1)S(1)}, bf16[2048,64]{0,1:T(8,128)(2,1)}, u32[]{:S(2)}) copy-start(bf16[2048,64]{0,1:T(8,128)(2,1)} %param.8) | copy-start | bytes 786436
  214.9 33.5 %copy-start.8 = (s32[8192,3]{0,1:T(4,128)S(1)}, s32[8192,3]{0,1:T(4,128)}, u32[]{:S(2)}) copy-start(s32[8192,3]{0,1:T(4,128)} %param.9) | copy-start | bytes 294916
  214.9 87.9 %all-gather.11.cloned.1.call-start = ((), (), s32[]{:S(2)}) async-start(), calls=%async_computation.18 | async-start | bytes 1310720 | tf_op jit(solution)/shard_map/all_gather | solution.py:27
  248.3 25.1 %copy-start.2 = (bf16[2048,64]{0,1:T(8,128)(2,1)}, bf16[2048,64]{0,1:T(8,128)(2,1)S(1)}, u32[]{:S(2)}) copy-start(bf16[2048,64]{0,1:T(8,128)(2,1)S(1)} %get-tuple-element.18) | copy-start | bytes 786436
  248.3 88.2 %reduce-scatter.21.cloned.1.call-start = ((), (), s32[]{:S(2)}) async-start(), calls=%async_computation.19 | async-start | bytes 786432 | tf_op jit(solution)/shard_map/reduce_scatter | solution.py:29
  324.7 212.0 %all-reduce.2.cloned.1.call-start = ((), (), s32[]{:S(2)}) async-start(), calls=%async_computation.21 | async-start | bytes 25165824 | tf_op jit(solution)/shard_map/psum | solution.py:64
  325.2 11.4 %copy-start.4 = (f32[1024,64]{0,1:T(8,128)S(1)}, f32[1024,64]{0,1:T(8,128)}, u32[]{:S(2)}) copy-start(f32[1024,64]{0,1:T(8,128)} %reduce-scatter.13.cloned.1.call-done) | copy-start | bytes 786436
  325.2 11.4 %copy-start.5 = (f32[1024,64]{0,1:T(8,128)S(1)}, f32[1024,64]{0,1:T(8,128)}, u32[]{:S(2)}) copy-start(f32[1024,64]{0,1:T(8,128)} %reduce-scatter.17.cloned.1.call-done) | copy-start | bytes 786436
  337.6 24.2 %copy-start.7 = (bf16[1024,64]{0,1:T(8,128)(2,1)}, bf16[1024,64]{0,1:T(8,128)(2,1)S(1)}, u32[]{:S(2)}) copy-start(bf16[1024,64]{0,1:T(8,128)(2,1)S(1)} %multiply_convert_fusion.3) | copy-start | bytes 393220
  361.9 2.5 copy-start
  376.2 334.3 %reduce-scatter.31.cloned.1.call-start = ((), (), s32[]{:S(2)}) async-start(), calls=%async_computation.27 | async-start | bytes 2621440 | tf_op jit(solution)/shard_map/reduce_scatter | solution.py:34
  613.7 112.8 %all-gather.13.cloned.1.call-start = ((), (), s32[]{:S(2)}) async-start(), calls=%async_computation.22 | async-start | bytes 1310720 | tf_op jit(solution)/shard_map/all_gather | solution.py:27
  712.4 36.3 %all-gather.17.cloned.1.call-start = ((), (), s32[]{:S(2)}) async-start(), calls=%async_computation.28 | async-start | bytes 1310720 | tf_op jit(solution)/shard_map/all_gather | solution.py:27
  713.1 57.5 %reduce-scatter.25.cloned.1.call-start = ((), (), s32[]{:S(2)}) async-start(), calls=%async_computation.23 | async-start | bytes 786432 | tf_op jit(solution)/shard_map/reduce_scatter | solution.py:29
  748.4 34.1 %reduce-scatter.33.cloned.1.call-start = ((), (), s32[]{:S(2)}) async-start(), calls=%async_computation.29 | async-start | bytes 786432 | tf_op jit(solution)/shard_map/reduce_scatter | solution.py:29
  770.5 59.2 %reduce-scatter.27.cloned.1.call-start = ((), (), s32[]{:S(2)}) async-start(), calls=%async_computation.24 | async-start | bytes 2621440 | tf_op jit(solution)/shard_map/reduce_scatter | solution.py:34
  804.1 53.5 %reduce-scatter.35.cloned.1.call-start = ((), (), s32[]{:S(2)}) async-start(), calls=%async_computation.30 | async-start | bytes 2621440 | tf_op jit(solution)/shard_map/reduce_scatter | solution.py:34
  824.7 49.0 %all-gather.15.cloned.1.call-start = ((), (), s32[]{:S(2)}) async-start(), calls=%async_computation.25 | async-start | bytes 1310720 | tf_op jit(solution)/shard_map/all_gather | solution.py:27
  859.8 47.7 %reduce-scatter.29.cloned.1.call-start = ((), (), s32[]{:S(2)}) async-start(), calls=%async_computation.26 | async-start | bytes 786432 | tf_op jit(solution)/shard_map/reduce_scatter | solution.py:29
Sparse Core Ops, SparseCore 0:
  9.5 16.5 all-gather.6
  99.8 25.5 reduce-scatter.14
  128.2 11.7 reduce-scatter.12
  142.0 13.6 all-gather.8
  177.7 11.7 reduce-scatter.16
  192.7 25.5 reduce-scatter.18
  220.7 25.5 reduce-scatter.22
  248.5 13.7 all-gather.10
  324.8 11.7 reduce-scatter.20
  376.3 160.3 all-reduce.1
  613.8 25.7 reduce-scatter.30
  712.5 13.9 all-gather.12
  728.6 13.7 all-gather.16
  748.5 11.7 reduce-scatter.24
  770.7 11.7 reduce-scatter.32
  804.2 25.5 reduce-scatter.26
  832.1 25.4 reduce-scatter.34
  859.9 13.7 all-gather.14
  895.7 11.7 reduce-scatter.28
where the time goes:
time: 926 us; the launch traced here: 917 us
  waiting for transfers between devices  304 us (33%)
  other arithmetic  244 us (26%)
  matrix products  221 us (24%)
  local copies, waits for them, and re-layouts  78.5 us (8%)
  blocking collectives  52.3 us (6%)
  between operations  16.5 us (2%)
    psum x1, waiting for transfers between devices, local_fn(): lax.psum(jnp.concatenate([rows_user, rows_pos, rows_neg], axis=0), ('row'...  160 us
    dot_general x6, matrix products, user_half(): partial_sum = jnp.dot(adj_blk, gathered, preferred_element_type=jnp.float32)  131 us
    scatter-add x1, other arithmetic, local_fn(): jax.ops.segment_sum(jnp.concatenate([grad_epos, -grad_epos], axis=0), jnp...  90.7 us
    dot_general x6, matrix products, item_half(): lax.dot_general(adj_blk, gathered, (((0,), (0,)), ((), ())), preferred_el...  89.4 us
    gather x3, local copies, waits for them, and re-layouts, lookup_rows(): jnp.take(emb_table, jnp.clip(local_ids, 0, emb_table.shape[0] - 1), axis=0)  77.5 us
    reduce_scatter x6, waiting for transfers between devices, item_half(): return lax.psum_scatter(partial_sum, 'row', scatter_dimension=0, tiled=True)  67.5 us
    scatter-add x1, other arithmetic, local_fn(): seed_user = jax.ops.segment_sum(grad_eu, seg_user, num_segments=user_rows)  48.8 us
    reduce_scatter x6, waiting for transfers between devices, user_half(): return lax.psum_scatter(partial_sum, 'col', scatter_dimension=0, tiled=True)  38 us
  transfers between devices with their start and end apart: 19, of which 13 were waited for; matrix products, arithmetic and copies ran while one was open for 37% of the time, Pallas kernels for 0%

commit v1 on v0

v1 whole, which is shorter than its diff:
```python
import jax
import jax.numpy as jnp
from jax import lax
from jax.experimental import pallas as pl
from jax.experimental.pallas import tpu as pltpu
from jax.sharding import PartitionSpec as P

MESH = pl.DeviceIdType.MESH
F32 = jnp.float32
BF16 = jnp.bfloat16

D = 64
UB = 1024
IB = 2048
RU = 2048
CI = 8192
STEPS = 3
SX = 4
WX = IB // SX
SY = 2
WY = UB // SY
TB = 1024
NT = 8192
PU = UB // 2
PI = IB // 2
PR = PU + PI

FD, XR, FO, GP, GX, GF, YR, YG = range(8)
VMEM_LIMIT = 67043328


def _coords():
    c = lax.axis_index('col')
    r = lax.axis_index('row')
    x = r // 2
    h = r % 2
    return c, r, x, h


def _dot(a, b):
    return lax.dot_general(a, b, (((1,), (0,)), ((), ())), preferred_element_type=F32)


def _dot_t(a, b):
    return lax.dot_general(a, b, (((1,), (1,)), ((), ())), preferred_element_type=F32)


def _al(v, m):
    return pl.multiple_of(v, m)


class Links:
    def __init__(self):
        self.c, self.r, self.x, self.h = _coords()
        c, r, x, h = self.c, self.r, self.x, self.h
        self.partner = (c, 2 * x + (1 - h))
        self.xn = (c, 2 * (1 - x) + h)
        self.yn = (1 - c, r)
        self.diag = (1 - c, 2 * (1 - x) + h)
        self.xpartner = (c, 2 * (1 - x) + (1 - h))
        self.slot = r * 2 + c

    def barrier(self):
        sem = pltpu.get_barrier_semaphore()
        peers = (self.partner, self.xn, self.yn, self.diag, self.xpartner)
        for p in peers:
            pl.semaphore_signal(sem, inc=1, device_id=p, device_id_type=MESH)
        pl.semaphore_wait(sem, len(peers))


def _slot_of(dev):
    return dev[1] * 2 + dev[0]


def _remote(src, dst, ss, rs, dev):
    return pltpu.make_async_remote_copy(src_ref=src, dst_ref=dst, send_sem=ss, recv_sem=rs, device_id=dev, device_id_type=MESH)


class Prop:
    def __init__(self, lk, a, ei, eu, pi, pu, rf, ro, rx, ry, ss, rs):
        self.lk = lk
        self.a, self.ei, self.eu, self.pi, self.pu = a, ei, eu, pi, pu
        self.rf, self.ro, self.rx, self.ry = rf, ro, rx, ry
        self.ss, self.rs = ss, rs

    def msg(self, kind, k, s):
        lk = self.lk
        ss, rs = self.ss.at[k, kind, s], self.rs.at[k, kind, s]
        other = 1 - lk.x
        if kind == FD:
            src = self.pi.at[:, pl.ds(_al((2 * other + 1 - lk.h) * IB + s * WX, 128), WX)]
            dst = self.rf.at[k, :, pl.ds(_al(s * WX, 128), WX)]
            return _remote(src, dst, ss, rs, lk.partner)
        if kind == XR:
            src = self.pi.at[:, pl.ds(_al((2 * other + lk.h) * IB + s * WX, 128), WX)]
            dst = self.rx.at[k, :, pl.ds(_al(s * WX, 128), WX)]
            return _remote(src, dst, ss, rs, lk.xn)
        if kind == FO:
            src = self.pi.at[:, pl.ds(_al((2 * lk.x + 1 - lk.h) * IB + s * WX, 128), WX)]
            dst = self.ro.at[k, :, pl.ds(_al(s * WX, 128), WX)]
            return _remote(src, dst, ss, rs, lk.partner)
        if kind in (GP, GX):
            ref = self.ei.at[k, :, pl.ds(_al(lk.r * IB + s * WX, 128), WX)]
            return _remote(ref, ref, ss, rs, lk.partner if kind == GP else lk.xn)
        if kind == GF:
            ref = self.ei.at[k, :, pl.ds(_al((2 * other + lk.h) * IB + s * WX, 128), WX)]
            return _remote(ref, ref, ss, rs, lk.partner)
        if kind == YR:
            src = self.pu.at[:, pl.ds(_al((1 - lk.c) * UB + s * WY, 128), WY)]
            dst = self.ry.at[k, :, pl.ds(_al(s * WY, 128), WY)]
            return _remote(src, dst, ss, rs, lk.yn)
        ref = self.eu.at[k, :, pl.ds(_al(lk.c * UB + s * WY, 128), WY)]
        return _remote(ref, ref, ss, rs, lk.yn)

    def put_item(self, k, s, value):
        self.ei[k, :, pl.ds(_al(self.lk.r * IB + s * WX, 128), WX)] = value
        self.msg(GX, k, s).start()
        self.msg(GP, k, s).start()

    def put_user(self, k, s, value):
        self.eu[k, :, pl.ds(_al(self.lk.c * UB + s * WY, 128), WY)] = value
        self.msg(YG, k, s).start()

    def wait_puts(self, k):
        for s in range(SX):
            self.msg(GX, k, s).wait_send()
            self.msg(GP, k, s).wait_send()
            self.msg(GF, k, s).wait_send()
        for s in range(SY):
            self.msg(YG, k, s).wait_send()

    def step(self, k, user_final, item_final):
        lk = self.lk
        a, ei, eu, pi, pu = self.a, self.ei, self.eu, self.pi, self.pu
        far = (1 - lk.x) * 2 * IB
        near = lk.x * 2 * IB
        own_u = lk.c * UB
        peer_u = (1 - lk.c) * UB

        if k > 0:
            for s in range(SX):
                self.msg(FD, k - 1, s).wait_send()
                self.msg(XR, k - 1, s).wait_send()

        def far_own(j, _):
            cols = pl.ds(_al(far + j * 1024, 128), 1024)
            pi[:, cols] = _dot(eu[k, :, pl.ds(_al(own_u, 128), UB)], a[pl.ds(_al(own_u, 128), UB), cols])
            return 0

        lax.fori_loop(0, 4, far_own, 0)
        for s in range(SY):
            self.msg(YG, k, s).wait_recv()

        def chip_sum(s):
            self.msg(FD, k, s).wait_recv()
            cols = pl.ds(_al((2 * (1 - lk.x) + lk.h) * IB + s * WX, 128), WX)
            pi[:, cols] = pi[:, cols] + self.rf[k, :, pl.ds(_al(s * WX, 128), WX)]
            self.msg(XR, k, s).start()

        def far_peer(s, _):
            e = eu[k, :, pl.ds(_al(peer_u, 128), UB)]
            rows = pl.ds(_al(peer_u, 128), UB)
            c1 = pl.ds(_al(far + (1 - lk.h) * IB + s * WX, 128), WX)
            c2 = pl.ds(_al(far + lk.h * IB + s * WX, 128), WX)
            pi[:, c1] = pi[:, c1] + _dot(e, a[rows, c1])
            pi[:, c2] = pi[:, c2] + _dot(e, a[rows, c2])
            self.msg(FD, k, s).start()

            @pl.when(s >= 1)
            def _():
                chip_sum(s - 1)
            return 0

        lax.fori_loop(0, SX, far_peer, 0)

        if k > 0:
            for s in range(SY):
                self.msg(YR, k - 1, s).wait_send()

        def near_items(j, _):
            rows = pl.ds(_al(j * 512, 512), 512)
            cols = pl.ds(_al(near, 128), 2 * IB)
            pu[:, pl.ds(_al(j * 512, 128), 512)] = _dot_t(ei[k, :, cols], a[rows, cols])

            @pl.when(j == 0)
            def _():
                chip_sum(SX - 1)
            self.msg(GX, k, j).wait_recv()
            self.msg(GF, k, j).start()
            return 0

        for s in range(SX):
            self.msg(GP, k, s).wait_recv()
        lax.fori_loop(0, 4, near_items, 0)
        for s in range(SX):
            self.msg(GF, k, s).wait_recv()

        def far_items(j, _):
            half = j // 2
            base = half * own_u + (1 - half) * peer_u + (j % 2) * WY
            rows = pl.ds(_al(base, 512), WY)
            cols = pl.ds(_al(far, 128), 2 * IB)
            uc = pl.ds(_al(base, 128), WY)
            pu[:, uc] = pu[:, uc] + _dot_t(ei[k, :, cols], a[rows, cols])

            @pl.when(j < SY)
            def _():
                self.msg(YR, k, j).start()
            return 0

        lax.fori_loop(0, 4, far_items, 0)

        if k > 0:
            for s in range(SX):
                self.msg(FO, k - 1, s).wait_send()

        def near_items_t(s, _):
            e = eu[k]
            c1 = pl.ds(_al(near + (1 - lk.h) * IB + s * WX, 128), WX)
            c2 = pl.ds(_al(near + lk.h * IB + s * WX, 128), WX)
            pi[:, c1] = _dot(e, a[:, c1])
            self.msg(FO, k, s).start()
            pi[:, c2] = _dot(e, a[:, c2])
            return 0

        lax.fori_loop(0, SX, near_items_t, 0)

        for s in range(SY):
            self.msg(YR, k, s).wait_recv()
            uc = pl.ds(_al(own_u + s * WY, 128), WY)
            user_final(k, s, pu[:, uc] + self.ry[k, :, s * WY:(s + 1) * WY])
        for s in range(SX):
            self.msg(FO, k, s).wait_recv()
            self.msg(XR, k, s).wait_recv()
            c2 = pl.ds(_al(near + lk.h * IB + s * WX, 128), WX)
            piece = slice(s * WX, (s + 1) * WX)
            item_final(k, s, (pi[:, c2] + self.ro[k, :, piece]) + self.rx[k, :, piece])

    def finish(self):
        k = STEPS - 1
        for s in range(SX):
            self.msg(FD, k, s).wait_send()
            self.msg(XR, k, s).wait_send()
            self.msg(FO, k, s).wait_send()
        for s in range(SY):
            self.msg(YR, k, s).wait_send()
        for k in range(STEPS):
            self.wait_puts(k)


class AllGather:
    def __init__(self, lk, ref, rows, ss, rs):
        self.lk, self.ref, self.rows, self.ss, self.rs = lk, ref, rows, ss, rs

    def _copy(self, i):
        lk = self.lk
        own = lk.slot
        xs, ys, ds_ = _slot_of(lk.xn), _slot_of(lk.yn), _slot_of(lk.diag)
        src_slot = (own, own, own, own, xs, ys, ds_)[i]
        dev = (lk.partner, lk.xn, lk.yn, lk.diag, lk.partner, lk.partner, lk.partner)[i]
        ref = self.ref.at[src_slot, self.rows]
        return _remote(ref, ref, self.ss.at[i], self.rs.at[i], dev)

    def start(self):
        for i in (1, 2, 0, 3):
            self._copy(i).start()

    def arrive(self, i):
        self._copy(i).wait_recv()
        if i in (1, 2, 3):
            self._copy(i + 3).start()

    def slot(self, i):
        lk = self.lk
        c, x, h = lk.c, lk.x, lk.h
        row = (2 * x + 1 - h, 2 * (1 - x) + h, lk.r, 2 * (1 - x) + h,
               2 * (1 - x) + 1 - h, 2 * x + 1 - h, 2 * (1 - x) + 1 - h)[i]
        col = (c, c, 1 - c, 1 - c, c, 1 - c, 1 - c)[i]
        return row * 2 + col

    def drain(self):
        for i in range(7):
            self._copy(i).wait_send()


ORDER = (0, 1, 2, 4, 5, 3, 6)


def _unpack_t(xt):
    n = xt.shape[1] // 2
    return jnp.concatenate([xt[:, :n], xt[:, n:]], axis=0).T


PROP_SCRATCH = [
    pltpu.VMEM((RU, CI), BF16),
    pltpu.VMEM((STEPS, D, CI), BF16),
    pltpu.VMEM((STEPS, D, RU), BF16),
    pltpu.VMEM((D, CI), F32),
    pltpu.VMEM((D, RU), F32),
    pltpu.VMEM((STEPS, D, IB), F32),
    pltpu.VMEM((STEPS, D, IB), F32),
    pltpu.VMEM((STEPS, D, IB), F32),
    pltpu.VMEM((STEPS, D, UB), F32),
    pltpu.SemaphoreType.DMA((STEPS, 8, 4)),
    pltpu.SemaphoreType.DMA((STEPS, 8, 4)),
]

CH = 64
NBUF = 4
NCH = RU // CH
AW = 8


def forward_kernel(mask, e0u, e0i, out_u, out_i, table, a_hbm,
                   a, ei, eu, pi, pu, rf, ro, rx, ry, ss, rs,
                   mbuf, msem, csum, rpart, dcol, drow, dss, drs, su, si, uacc, iacc, asem, tss, trs, iss, irs):
    lk = Links()

    def mask_copy(j):
        slot = j % NBUF
        return pltpu.make_async_copy(mask.at[pl.ds(_al(j * CH, CH), CH), :], mbuf.at[slot], msem.at[slot])

    for j in range(NBUF):
        mask_copy(j).start()
    lk.barrier()
    pr = Prop(lk, a, ei, eu, pi, pu, rf, ro, rx, ry, ss, rs)

    iacc[...] = e0i[...].astype(F32)
    for s in range(SX):
        pr.put_item(0, s, e0i[:, s * WX:(s + 1) * WX])
    uacc[...] = e0u[...].astype(F32)
    for s in range(SY):
        pr.put_user(0, s, e0u[:, s * WY:(s + 1) * WY])

    csum[...] = jnp.zeros_like(csum)

    def chunk(j, _):
        slot = j % NBUF
        mask_copy(j).wait()
        rows = pl.ds(_al(j * CH, CH), CH)

        def cols_body(w, acc):
            cols = pl.ds(_al(w * 512, 512), 512)
            v = mbuf[slot, :, cols].astype(F32)
            a[rows, cols] = v.astype(BF16)
            csum[:, cols] = csum[:, cols] + jnp.sum(v.reshape(CH // 8, 8, 512), axis=0)
            return acc + ((v[:, 0:128] + v[:, 128:256]) + (v[:, 256:384] + v[:, 384:512]))

        rpart[rows, :] = lax.fori_loop(0, CI // 512, cols_body, jnp.zeros((CH, 128), F32))

        @pl.when(j + NBUF < NCH)
        def _():
            mask_copy(j + NBUF).start()
        return 0

    lax.fori_loop(0, NCH, chunk, 0)

    ctot = jnp.sum(csum[...], axis=0, keepdims=True)
    for j in range(8):
        dcol[0, j:j + 1, :] = ctot[:, j * 1024:(j + 1) * 1024]
    drow[0] = _dot_t(jnp.ones((8, 128), BF16), rpart[...].astype(BF16))
    dcopies = [_remote(dcol.at[0], dcol.at[1 + i], dss.at[i], drs.at[i], dev)
               for i, dev in enumerate((lk.partner, lk.xn, lk.xpartner))]
    dcopies.append(_remote(drow.at[0], drow.at[1], dss.at[3], drs.at[3], lk.yn))
    for cp in dcopies:
        cp.start()
    for cp in dcopies:
        cp.wait_recv()
    ctot8 = (dcol[0] + dcol[1]) + (dcol[2] + dcol[3])
    sc8 = lax.rsqrt(jnp.maximum(ctot8, 1.0))
    for j in range(8):
        si[:, j * 1024:(j + 1) * 1024] = sc8[j:j + 1, :]
    su8 = lax.rsqrt(jnp.maximum(drow[0] + drow[1], 1.0))
    for j in range(RU // 128):
        su[j * 128:(j + 1) * 128, :] = jnp.broadcast_to(su8[0:1, j * 128:(j + 1) * 128], (128, 128)).T

    def a_copy(j):
        rows = pl.ds(_al(j * (RU // AW), RU // AW), RU // AW)
        return pltpu.make_async_copy(a.at[rows, :], a_hbm.at[rows, :], asem.at[j])

    def scale_rows(m, _):
        rows = pl.ds(_al(m * 64, 64), 64)
        s = su[rows, :]
        s4 = jnp.concatenate([s, s, s, s], axis=1)

        def scale_cols(w, _):
            cols = pl.ds(_al(w * 512, 512), 512)
            a[rows, cols] = ((s4 * a[rows, cols].astype(F32)) * si[:, cols]).astype(BF16)
            return 0

        lax.fori_loop(0, CI // 512, scale_cols, 0)
        return 0

    for j in range(AW):
        n = RU // AW // 64
        lax.fori_loop(j * n, (j + 1) * n, scale_rows, 0)
        a_copy(j).start()

    def user_final(k, s, v):
        b = v.astype(BF16)
        if k < STEPS - 1:
            pr.put_user(k + 1, s, b)
        uacc[:, s * WY:(s + 1) * WY] = uacc[:, s * WY:(s + 1) * WY] + b.astype(F32)
        if k == STEPS - 1 and s == SY - 1:
            t = uacc[...] * 0.25
            table[lk.slot, 0:PU, :] = _unpack_t(t).astype(BF16)
            ag_u.start()
            out_u[...] = t.astype(BF16)

    def item_final(k, s, v):
        b = v.astype(BF16)
        if k < STEPS - 1:
            pr.put_item(k + 1, s, b)
        iacc[:, s * WX:(s + 1) * WX] = iacc[:, s * WX:(s + 1) * WX] + b.astype(F32)
        if k == STEPS - 1 and s == SX - 1:
            t = iacc[...] * 0.25
            table[lk.slot, PU:PR, :] = _unpack_t(t).astype(BF16)
            ag_i.start()
            out_i[...] = t.astype(BF16)

    ag_u = AllGather(lk, table, pl.ds(0, PU), tss, trs)
    ag_i = AllGather(lk, table, pl.ds(PU, PI), iss, irs)
    for k in range(STEPS):
        pr.step(k, user_final, item_final)
    for ag in (ag_u, ag_i):
        for i in ORDER:
            ag.arrive(i)
    for cp in dcopies:
        cp.wait_send()
    for j in range(AW):
        a_copy(j).wait()
    pr.finish()
    ag_u.drain()
    ag_i.drain()


def lookup_kernel(table, ru, rp, rn, out, tab, gu, gp, gn):
    def unpack(b, _):
        for lo, n, dst in ((0, PU, 0), (PU, PI, UB)):
            for o in range(0, n, 128):
                v = table[b, lo + o:lo + o + 128, :].astype(F32)
                base = b * (UB + IB) + dst + o
                tab[pl.ds(_al(base, 128), 128), :] = v
                tab[pl.ds(_al(base + n, 128), 128), :] = pltpu.roll(v, D, 1)
        return 0

    lax.fori_loop(0, 8, unpack, 0)

    def gather(g, _):
        for o in range(8):
            t = g * 8 + o
            gu[pl.ds(t, 1), :] = tab[pl.ds(ru[t], 1), :]
            gp[pl.ds(t, 1), :] = tab[pl.ds(rp[t], 1), :]
            gn[pl.ds(t, 1), :] = tab[pl.ds(rn[t], 1), :]
        return 0

    lax.fori_loop(0, TB // 8, gather, 0)

    def block(m, tot):
        rows = pl.ds(_al(m * 128, 128), 128)
        left = lax.broadcasted_iota(jnp.int32, (128, 128), 1) < D
        e_u = gu[rows, :]
        e_d = gp[rows, :] - gn[rows, :]
        x = jnp.sum(jnp.where(left, e_u * e_d, 0.0), axis=1, keepdims=True)
        z = jnp.exp(-jnp.abs(x))
        loss = jnp.maximum(-x, 0.0) + jnp.log1p(z)
        sig = jnp.where(x >= 0.0, z, 1.0) / (1.0 + z)
        coef = sig * (-1.0 / NT)
        out[rows, :] = jnp.where(left, coef * e_d, pltpu.roll(coef * e_u, D, 1))
        return tot + jnp.sum(loss, axis=0, keepdims=True)

    tot = lax.fori_loop(0, TB // 128, block, jnp.zeros((1, 1), F32))
    out[TB:TB + 8, :] = jnp.broadcast_to(tot, (8, 128))


def backward_kernel(a_hbm, g_in, uid, pid, nid, out_u, out_i, out_l,
                    a, ei, eu, pi, pu, rf, ro, rx, ry, ss, rs,
                    asem, g_all, gsem, gss, grs, wu, wi, acc_u, acc_i, su, si):
    lk = Links()
    loads = [pltpu.make_async_copy(a_hbm, a, asem)]
    gcopy = pltpu.make_async_copy(g_in, g_all.at[lk.slot], gsem)
    gcopy.start()
    loads[0].start()
    lk.barrier()
    pr = Prop(lk, a, ei, eu, pi, pu, rf, ro, rx, ry, ss, rs)
    gcopy.wait()
    ag = AllGather(lk, g_all, pl.ds(0, TB + 8), gss, grs)
    ag.start()
    acc_u[...] = jnp.zeros_like(acc_u)
    acc_i[...] = jnp.zeros_like(acc_i)
    base_u = lk.slot * UB
    base_i = (lk.c * 4 + lk.r) * IB

    def scatter(b):
        def split(m, _):
            rows = pl.ds(_al(m * 128, 128), 128)
            left = lax.broadcasted_iota(jnp.int32, (128, 128), 1) < D
            g = g_all[b, rows, :]
            hi = g.astype(BF16).astype(F32)
            r1 = g - hi
            mid = r1.astype(BF16).astype(F32)
            lo = r1 - mid
            wu[rows, 0:128] = jnp.where(left, hi, pltpu.roll(mid, D, 1)).astype(BF16)
            wu[rows, 128:256] = lo.astype(BF16)
            wi[rows, 0:128] = jnp.where(left, pltpu.roll(hi, D, 1), mid).astype(BF16)
            wi[rows, 128:256] = pltpu.roll(lo, D, 1).astype(BF16)
            return 0

        lax.fori_loop(0, TB // 128, split, 0)
        cols = pl.ds(_al(b * TB, 128), TB)

        def users(m, _):
            ids = lax.broadcasted_iota(jnp.int32, (256, TB), 0) + (base_u + m * 256)
            hot = jnp.where(ids == uid[:, cols], 1.0, 0.0).astype(BF16)
            rows = pl.ds(_al(m * 256, 256), 256)
            acc_u[rows, :] = acc_u[rows, :] + _dot(hot, wu[...])
            return 0

        def items(m, _):
            ids = lax.broadcasted_iota(jnp.int32, (256, TB), 0) + (base_i + m * 256)
            hot = (jnp.where(ids == pid[:, cols], 1.0, 0.0) - jnp.where(ids == nid[:, cols], 1.0, 0.0)).astype(BF16)
            rows = pl.ds(_al(m * 256, 256), 256)
            acc_i[rows, :] = acc_i[rows, :] + _dot(hot, wi[...])
            return 0

        lax.fori_loop(0, UB // 256, users, 0)
        lax.fori_loop(0, IB // 256, items, 0)

    scatter(lk.slot)
    for i in ORDER:
        ag.arrive(i)
        scatter(ag.slot(i))

    loss = g_all[0, TB:TB + 8, :]
    for b in range(1, 8):
        loss = loss + g_all[b, TB:TB + 8, :]
    out_l[...] = loss * (1.0 / NT)

    def seed(acc):
        s = (acc[:, 0:128] + pltpu.roll(acc[:, 0:128], D, 1)) + acc[:, 128:256]
        n = s.shape[0] // 2
        s = s * 0.25
        left = lax.broadcasted_iota(jnp.int32, (n, 128), 1) < D
        return jnp.where(left, s[:n], pltpu.roll(s[n:], D, 1)).T

    xi = seed(acc_i[...])
    for s in range(SX):
        src = xi[:D] if s < SX // 2 else xi[D:]
        o = (s % (SX // 2)) * WX
        v = src[:, o:o + WX]
        si[:, s * WX:(s + 1) * WX] = v
        pr.put_item(0, s, v.astype(BF16))
    xu = seed(acc_u[...])
    for s in range(SY):
        v = xu[:D] if s == 0 else xu[D:]
        su[:, s * WY:(s + 1) * WY] = v
        pr.put_user(0, s, v.astype(BF16))

    def user_final(k, s, v):
        v = su[:, s * WY:(s + 1) * WY] + v
        if k < STEPS - 1:
            pr.put_user(k + 1, s, v.astype(BF16))
        else:
            out_u[:, s * WY:(s + 1) * WY] = v

    def item_final(k, s, v):
        v = si[:, s * WX:(s + 1) * WX] + v
        if k < STEPS - 1:
            pr.put_item(k + 1, s, v.astype(BF16))
        else:
            out_i[:, s * WX:(s + 1) * WX] = v

    loads[0].wait()
    for k in range(STEPS):
        pr.step(k, user_final, item_final)
    pr.finish()
    ag.drain()


VM = pl.BlockSpec(memory_space=pltpu.VMEM)
SM = pl.BlockSpec(memory_space=pltpu.SMEM)
ANY = pl.BlockSpec(memory_space=pl.ANY)
DMA = pltpu.SemaphoreType.DMA


def _params(cid):
    return pltpu.CompilerParams(collective_id=cid, has_side_effects=True, vmem_limit_bytes=VMEM_LIMIT)


def solution(mesh):
    def local_fn(mask, e0u, e0i, triples):
        c, r, _, _ = _coords()
        slot = r * 2 + c
        out_u, out_i, table, a_hbm = pl.pallas_call(
            forward_kernel,
            name='forward',
            out_shape=(jax.ShapeDtypeStruct((D, UB), BF16), jax.ShapeDtypeStruct((D, IB), BF16),
                       jax.ShapeDtypeStruct((8, PR, 128), BF16), jax.ShapeDtypeStruct((RU, CI), BF16)),
            in_specs=[ANY, VM, VM],
            out_specs=(VM, VM, VM, ANY),
            scratch_shapes=PROP_SCRATCH + [
                pltpu.VMEM((NBUF, CH, CI), jnp.int32), DMA((NBUF,)),
                pltpu.VMEM((8, CI), F32), pltpu.VMEM((RU, 128), F32),
                pltpu.VMEM((4, 8, 1024), F32), pltpu.VMEM((2, 8, RU), F32), DMA((4,)), DMA((4,)),
                pltpu.VMEM((RU, 128), F32), pltpu.VMEM((1, CI), F32),
                pltpu.VMEM((D, UB), F32), pltpu.VMEM((D, IB), F32), DMA((AW,)),
                DMA((7,)), DMA((7,)), DMA((7,)), DMA((7,)),
            ],
            compiler_params=_params(0),
        )(mask, e0u.T, e0i.T)

        cols = triples.T
        mine = lax.dynamic_slice(cols, (0, slot * TB), (3, TB))
        per = UB + IB
        row_u = (mine[0] // UB) * per + mine[0] % UB
        blk = mine[1:] // IB
        row_i = ((blk % 4) * 2 + blk // 4) * per + UB + mine[1:] % IB
        g = pl.pallas_call(
            lookup_kernel,
            name='lookup',
            out_shape=jax.ShapeDtypeStruct((TB + 8, 128), F32),
            in_specs=[VM, SM, SM, SM],
            out_specs=VM,
            scratch_shapes=[pltpu.VMEM((8 * per, 128), F32)] + [pltpu.VMEM((TB, 128), F32)] * 3,
            compiler_params=pltpu.CompilerParams(vmem_limit_bytes=40 * 1024 * 1024),
        )(table, row_u, row_i[0], row_i[1])

        d_u, d_i, loss = pl.pallas_call(
            backward_kernel,
            name='backward',
            out_shape=(jax.ShapeDtypeStruct((D, UB), F32), jax.ShapeDtypeStruct((D, IB), F32),
                       jax.ShapeDtypeStruct((8, 128), F32)),
            in_specs=[ANY, ANY, VM, VM, VM],
            out_specs=(VM, VM, VM),
            scratch_shapes=PROP_SCRATCH + [
                DMA, pltpu.VMEM((8, TB + 8, 128), F32), DMA, DMA((7,)), DMA((7,)),
                pltpu.VMEM((TB, 256), BF16), pltpu.VMEM((TB, 256), BF16),
                pltpu.VMEM((UB, 256), F32), pltpu.VMEM((IB, 256), F32),
                pltpu.VMEM((D, UB), F32), pltpu.VMEM((D, IB), F32),
            ],
            compiler_params=_params(1),
        )(a_hbm, g, cols[0:1], cols[1:2], cols[2:3])
        return out_u.T, out_i.T, loss[0, 0], d_u.T, d_i.T

    user_spec = P(('row', 'col'), None)
    item_spec = P(('col', 'row'), None)
    return jax.shard_map(local_fn, mesh=mesh, in_specs=(P('row', 'col'), user_spec, item_spec, P()),
                         out_specs=(user_spec, item_spec, P(), user_spec, item_spec), check_vma=False)
```

time: 926 us -> 285 us (0.31)
  waiting for transfers between devices: 304 us -> 0 us
  Pallas kernels: 0 us -> 270 us
  other arithmetic: 244 us -> 0.09 us
  matrix products: 221 us -> 0 us
  local copies, waits for them, and re-layouts: 78.5 us -> 13.2 us
  blocking collectives: 52.3 us -> 0 us
  between operations: 16.5 us -> 0.69 us
    pallas_call x0 -> x3, Pallas kernels: none -> 270 us  [the longest x1 133 us: local_fn(): pl.pallas_call(forward_kernel, name='forward', out_shape=(jax.ShapeDtypeS...]
    dot_general x12 -> x0, matrix products: 221 us -> none  [the longest x6 131 us: user_half(): partial_sum = jnp.dot(adj_blk, gathered, preferred_element_type=jnp.float32)]
    psum x1 -> x0, waiting for transfers between devices: 160 us -> none  [local_fn(): lax.psum(jnp.concatenate([rows_user, rows_pos, rows_neg], axis=0), ('row'...]
    scatter-add x2 -> x0, other arithmetic: 139 us -> none  [the longest x1 90.7 us: local_fn(): jax.ops.segment_sum(jnp.concatenate([grad_epos, -grad_epos], axis=0), jnp...]
    reduce_scatter x12 -> x0, waiting for transfers between devices: 106 us -> none  [the longest x6 67.5 us: item_half(): return lax.psum_scatter(partial_sum, 'row', scatter_dimension=0, tiled=True)]
    gather x3 -> x0, local copies, waits for them, and re-layouts: 77.5 us -> none  [lookup_rows(): jnp.take(emb_table, jnp.clip(local_ids, 0, emb_table.shape[0] - 1), axis=0)]
    convert_element_type x9 -> x0, other arithmetic: 42.4 us -> none  [the longest x1 32.7 us: local_fn(): (scale_user[:, None] * mask_blk.astype(jnp.float32) * scale_item[None, :]...]
    all_gather x6 -> x0, waiting for transfers between devices: 36.1 us -> none  [user_half(): gathered = lax.all_gather(item_shard, 'row', axis=0, tiled=True)]
  transfers between devices with their start and end apart: 19 -> 0, of which waited for: 13 -> 0; matrix products, arithmetic and copies ran while one was open for 37% -> 0% of each run, Pallas kernels for 0% -> 0%
where the time goes in v1:
time: 285 us; the launch traced here: 284 us
  Pallas kernels  270 us (95%)
  local copies, waits for them, and re-layouts  13.2 us (5%)
    pallas_call x1, Pallas kernels, local_fn(): pl.pallas_call(forward_kernel, name='forward', out_shape=(jax.ShapeDtypeS...  133 us
    pallas_call x1, Pallas kernels, local_fn(): pl.pallas_call(backward_kernel, name='backward', out_shape=(jax.ShapeDtyp...  131 us
    unnamed x8, local copies, waits for them, and re-layouts  9.46 us
    pallas_call x1, Pallas kernels, local_fn(): pl.pallas_call(lookup_kernel, name='lookup', out_shape=jax.ShapeDtypeStru...  6.28 us

profile of v1, /device:TPU:0, one launch (start us, length us, event | category | flops | bytes accessed | tf_op | source)
XLA Modules:
  0.0 284.3 jit_solution(10218878971208219301)
XLA Ops:
  0.6 133.4 %forward.1 = (bf16[64,1024]{1,0:T(8,128)(2,1)}, bf16[64,2048]{1,0:T(8,128)(2,1)}, bf16[8,1536,128]{2,1,0:T(8,128)(2,1)}, bf16[2048,8192]{1,0:T(8,128)(2,1)}) custom-call(s32[2048,8192]{1,0:T(8,128)} %mask.1, bf16[64,1024]{1,0:T(8,128)(2,1)} %bitcast.19, bf16[64,2048]{1,0:T(8,128)(2,1)} %bitcast.16), custom_call_target="tpu_custom_call" | custom-call | tf_op jit(solution)/shard_map/forward/pallas_call | solution.py:594
  134.0 0.7 dynamic-slice_bitcast_fusion
  134.7 0.1 fusion.2
  134.8 0.0 copy-start
  134.8 1.9 copy-done
  136.7 6.3 %lookup.1.g_in = f32[1032,128]{1,0:T(8,128)S(1)} custom-call(bf16[8,1536,128]{2,1,0:T(8,128)(2,1)S(1)} %copy-done, s32[1024]{0:T(1024)S(1)} %fusion.4.ru, s32[1024]{0:T(1024)S(1)} %bitcast.14, s32[1024]{0:T(1024)S(1)} %bitcast.13), custom_call_target="tpu_custom_call" | custom-call | tf_op jit(solution)/shard_map/lookup/pallas_call | solution.py:618
  143.0 0.0 copy-start.1
  143.0 0.8 copy-done.1
  143.8 1.8 fusion.9
  145.6 130.7 %backward.1 = (f32[64,1024]{1,0:T(8,128)}, f32[64,2048]{1,0:T(8,128)}, f32[8,128]{1,0:T(8,128)}) custom-call(bf16[2048,8192]{1,0:T(8,128)(2,1)} %get-tuple-element.14.a_hbm, f32[1032,128]{1,0:T(8,128)} %copy-done.1, s32[1,8192]{1,0:T(1,128)} %get-tuple-element.21.uid, s32[1,8192]{1,0:T(1,128)} %get-tuple-element.20.pid, s32[1,8192]{1,0:T(1,128)} %get-tuple-element.19.nid), custom_call_target="tpu_custom_call" | custom-call | tf_op jit(solution)/shard_map/backward/pallas_call | solution.py:628
  276.3 1.2 slice.33
  277.5 1.6 copy.13
  279.1 1.7 copy.14
  280.8 1.7 copy.15
  282.4 1.9 copy.16
  (3 shorter events, 0.0 us)
Async XLA Ops:
  134.8 1.9 copy-start
  143.0 0.8 copy-start.1

commit v2 on v1

--- a/solution.py
+++ b/solution.py
@@ -125,11 +125,12 @@
         for s in range(SX):
             self.msg(GX, k, s).wait_send()
             self.msg(GP, k, s).wait_send()
-            self.msg(GF, k, s).wait_send()
+            if k == STEPS - 1:
+                self.msg(GF, k, s).wait_send()
         for s in range(SY):
             self.msg(YG, k, s).wait_send()
 
-    def step(self, k, user_final, item_final):
+    def step(self, k, user_final, item_final, between=None):
         lk = self.lk
         a, ei, eu, pi, pu = self.a, self.ei, self.eu, self.pi, self.pu
         far = (1 - lk.x) * 2 * IB
@@ -137,10 +138,14 @@
         own_u = lk.c * UB
         peer_u = (1 - lk.c) * UB
 
+        def far_cols(piece, half):
+            return _al(far + half * IB + piece * 1024, 128)
+
         if k > 0:
             for s in range(SX):
                 self.msg(FD, k - 1, s).wait_send()
                 self.msg(XR, k - 1, s).wait_send()
+                self.msg(GF, k - 1, s).wait_send()
 
         def far_own(j, _):
             cols = pl.ds(_al(far + j * 1024, 128), 1024)
@@ -151,64 +156,33 @@
         for s in range(SY):
             self.msg(YG, k, s).wait_recv()
 
-        def chip_sum(s):
-            self.msg(FD, k, s).wait_recv()
-            cols = pl.ds(_al((2 * (1 - lk.x) + lk.h) * IB + s * WX, 128), WX)
-            pi[:, cols] = pi[:, cols] + self.rf[k, :, pl.ds(_al(s * WX, 128), WX)]
-            self.msg(XR, k, s).start()
-
-        def far_peer(s, _):
+        def far_peer(j, _):
             e = eu[k, :, pl.ds(_al(peer_u, 128), UB)]
             rows = pl.ds(_al(peer_u, 128), UB)
-            c1 = pl.ds(_al(far + (1 - lk.h) * IB + s * WX, 128), WX)
-            c2 = pl.ds(_al(far + lk.h * IB + s * WX, 128), WX)
-            pi[:, c1] = pi[:, c1] + _dot(e, a[rows, c1])
-            pi[:, c2] = pi[:, c2] + _dot(e, a[rows, c2])
-            self.msg(FD, k, s).start()
-
-            @pl.when(s >= 1)
-            def _():
-                chip_sum(s - 1)
-            return 0
-
-        lax.fori_loop(0, SX, far_peer, 0)
-
-        if k > 0:
-            for s in range(SY):
-                self.msg(YR, k - 1, s).wait_send()
-
-        def near_items(j, _):
-            rows = pl.ds(_al(j * 512, 512), 512)
-            cols = pl.ds(_al(near, 128), 2 * IB)
-            pu[:, pl.ds(_al(j * 512, 128), 512)] = _dot_t(ei[k, :, cols], a[rows, cols])
-
-            @pl.when(j == 0)
-            def _():
-                chip_sum(SX - 1)
-            self.msg(GX, k, j).wait_recv()
-            self.msg(GF, k, j).start()
-            return 0
-
-        for s in range(SX):
-            self.msg(GP, k, s).wait_recv()
-        lax.fori_loop(0, 4, near_items, 0)
-        for s in range(SX):
-            self.msg(GF, k, s).wait_recv()
-
-        def far_items(j, _):
-            half = j // 2
-            base = half * own_u + (1 - half) * peer_u + (j % 2) * WY
-            rows = pl.ds(_al(base, 512), WY)
-            cols = pl.ds(_al(far, 128), 2 * IB)
-            uc = pl.ds(_al(base, 128), WY)
-            pu[:, uc] = pu[:, uc] + _dot_t(ei[k, :, cols], a[rows, cols])
-
-            @pl.when(j < SY)
-            def _():
-                self.msg(YR, k, j).start()
-            return 0
-
-        lax.fori_loop(0, 4, far_items, 0)
+            first = j < 2
+            half = jnp.where(first, 1 - lk.h, lk.h)
+            p = j % 2
+            cols = pl.ds(far_cols(p, half), 1024)
+            pi[:, cols] = pi[:, cols] + _dot(e, a[rows, cols])
+
+            @pl.when(first)
+            def _():
+                for q in range(2):
+                    self.msg(FD, k, 2 * p + q).start()
+
+            @pl.when(j >= 2)
+            def _():
+                for q in range(2):
+                    s = 2 * p + q
+                    self.msg(FD, k, s).wait_recv()
+                    cs = pl.ds(_al(far + lk.h * IB + s * WX, 128), WX)
+                    pi[:, cs] = pi[:, cs] + self.rf[k, :, pl.ds(_al(s * WX, 128), WX)]
+                    self.msg(XR, k, s).start()
+            return 0
+
+        lax.fori_loop(0, 4, far_peer, 0)
+        if between is not None:
+            between()
 
         if k > 0:
             for s in range(SX):
@@ -221,20 +195,79 @@
             pi[:, c1] = _dot(e, a[:, c1])
             self.msg(FO, k, s).start()
             pi[:, c2] = _dot(e, a[:, c2])
+            self.msg(GX, k, s).wait_recv()
+            self.msg(GF, k, s).start()
             return 0
 
         lax.fori_loop(0, SX, near_items_t, 0)
 
-        for s in range(SY):
+        if k > 0:
+            for s in range(SY):
+                self.msg(YR, k - 1, s).wait_send()
+        for s in range(SX):
+            self.msg(GP, k, s).wait_recv()
+
+        def item_piece(s):
+            self.msg(FO, k, s).wait_recv()
+            self.msg(XR, k, s).wait_recv()
+            c2 = pl.ds(_al(near + lk.h * IB + s * WX, 128), WX)
+            piece = pl.ds(_al(s * WX, 128), WX)
+            item_final(k, s, (pi[:, c2] + self.ro[k, :, piece]) + self.rx[k, :, piece])
+
+        def user_piece(s):
             self.msg(YR, k, s).wait_recv()
             uc = pl.ds(_al(own_u + s * WY, 128), WY)
             user_final(k, s, pu[:, uc] + self.ry[k, :, s * WY:(s + 1) * WY])
-        for s in range(SX):
-            self.msg(FO, k, s).wait_recv()
-            self.msg(XR, k, s).wait_recv()
-            c2 = pl.ds(_al(near + lk.h * IB + s * WX, 128), WX)
-            piece = slice(s * WX, (s + 1) * WX)
-            item_final(k, s, (pi[:, c2] + self.ro[k, :, piece]) + self.rx[k, :, piece])
+
+        def users_tile(t, _):
+            u = t // 2
+            is_far = t % 2
+            own = u // 2
+            base = own * own_u + (1 - own) * peer_u + (u % 2) * WY
+            at = is_far * far + (1 - is_far) * near
+            rows = pl.ds(_al(base, 512), WY)
+            uc = pl.ds(_al(base, 128), WY)
+            cols = pl.ds(_al(at, 128), 2 * IB)
+            v = _dot_t(ei[k, :, cols], a[rows, cols])
+
+            @pl.when(is_far == 0)
+            def _():
+                pu[:, uc] = v
+
+            @pl.when(t == 0)
+            def _():
+                for s in range(SX):
+                    self.msg(GF, k, s).wait_recv()
+
+            @pl.when(is_far == 1)
+            def _():
+                pu[:, uc] = pu[:, uc] + v
+
+            @pl.when(t == 1)
+            def _():
+                self.msg(YR, k, 0).start()
+
+            @pl.when(t == 2)
+            def _():
+                item_piece(0)
+
+            @pl.when(t == 3)
+            def _():
+                self.msg(YR, k, 1).start()
+
+            @pl.when(t == 4)
+            def _():
+                item_piece(1)
+
+            @pl.when(t == 6)
+            def _():
+                user_piece(0)
+                item_piece(2)
+            return 0
+
+        lax.fori_loop(0, 8, users_tile, 0)
+        user_piece(1)
+        item_piece(3)
 
     def finish(self):
         k = STEPS - 1
@@ -378,23 +411,28 @@
         rows = pl.ds(_al(j * (RU // AW), RU // AW), RU // AW)
         return pltpu.make_async_copy(a.at[rows, :], a_hbm.at[rows, :], asem.at[j])
 
-    def scale_rows(m, _):
-        rows = pl.ds(_al(m * 64, 64), 64)
-        s = su[rows, :]
-        s4 = jnp.concatenate([s, s, s, s], axis=1)
-
-        def scale_cols(w, _):
-            cols = pl.ds(_al(w * 512, 512), 512)
-            a[rows, cols] = ((s4 * a[rows, cols].astype(F32)) * si[:, cols]).astype(BF16)
-            return 0
-
-        lax.fori_loop(0, CI // 512, scale_cols, 0)
-        return 0
-
-    for j in range(AW):
-        n = RU // AW // 64
-        lax.fori_loop(j * n, (j + 1) * n, scale_rows, 0)
-        a_copy(j).start()
+    def scale(first_col):
+        def scale_rows(m, _):
+            rows = pl.ds(_al(m * 64, 64), 64)
+            s = su[rows, :]
+            s4 = jnp.concatenate([s, s, s, s], axis=1)
+
+            def scale_cols(w, _):
+                cols = pl.ds(_al(first_col + w * 512, 512), 512)
+                a[rows, cols] = a[rows, cols] * (s4 * si[:, cols]).astype(BF16)
+                return 0
+
+            lax.fori_loop(0, CI // 1024, scale_cols, 0)
+            return 0
+
+        lax.fori_loop(0, RU // 64, scale_rows, 0)
+
+    def scale_near():
+        scale(lk.x * 2 * IB)
+        for j in range(AW):
+            a_copy(j).start()
+
+    scale((1 - lk.x) * 2 * IB)
 
     def user_final(k, s, v):
         b = v.astype(BF16)
@@ -421,7 +459,7 @@
     ag_u = AllGather(lk, table, pl.ds(0, PU), tss, trs)
     ag_i = AllGather(lk, table, pl.ds(PU, PI), iss, irs)
     for k in range(STEPS):
-        pr.step(k, user_final, item_final)
+        pr.step(k, user_final, item_final, scale_near if k == 0 else None)
     for ag in (ag_u, ag_i):
         for i in ORDER:
             ag.arrive(i)
@@ -508,17 +546,23 @@
 
         lax.fori_loop(0, TB // 128, split, 0)
         cols = pl.ds(_al(b * TB, 128), TB)
+        sub = lax.broadcasted_iota(jnp.int32, (256, TB), 0).astype(F32).astype(BF16)
+        one, zero = jnp.array(1.0, BF16), jnp.array(0.0, BF16)
+
+        def lanes(ids, base):
+            v = ids[:, cols] - base
+            v = jnp.where((v >= 0) & (v < 256), v, -1).astype(F32)
+            return jnp.broadcast_to(v, (256, TB)).astype(BF16)
 
         def users(m, _):
-            ids = lax.broadcasted_iota(jnp.int32, (256, TB), 0) + (base_u + m * 256)
-            hot = jnp.where(ids == uid[:, cols], 1.0, 0.0).astype(BF16)
+            hot = jnp.where(lanes(uid, base_u + m * 256) == sub, one, zero)
             rows = pl.ds(_al(m * 256, 256), 256)
             acc_u[rows, :] = acc_u[rows, :] + _dot(hot, wu[...])
             return 0
 
         def items(m, _):
-            ids = lax.broadcasted_iota(jnp.int32, (256, TB), 0) + (base_i + m * 256)
-            hot = (jnp.where(ids == pid[:, cols], 1.0, 0.0) - jnp.where(ids == nid[:, cols], 1.0, 0.0)).astype(BF16)
+            hot_p = jnp.where(lanes(pid, base_i + m * 256) == sub, one, zero)
+            hot = hot_p - jnp.where(lanes(nid, base_i + m * 256) == sub, one, zero)
             rows = pl.ds(_al(m * 256, 256), 256)
             acc_i[rows, :] = acc_i[rows, :] + _dot(hot, wi[...])
             return 0

time: 285 us -> 266 us (0.933)
  Pallas kernels: 270 us -> 251 us
    pallas_call x1, Pallas kernels: 133 us -> 123 us  [local_fn(): pl.pallas_call(forward_kernel, name='forward', out_shape=(jax.ShapeDtypeS...]
    pallas_call x1, Pallas kernels: 131 us -> 122 us  [local_fn(): pl.pallas_call(backward_kernel, name='backward', out_shape=(jax.ShapeDtyp...]
where the time goes in v2:
time: 266 us; the launch traced here: 265 us
  Pallas kernels  251 us (94%)
  local copies, waits for them, and re-layouts  13.2 us (5%)
    pallas_call x1, Pallas kernels, local_fn(): pl.pallas_call(forward_kernel, name='forward', out_shape=(jax.ShapeDtypeS...  123 us
    pallas_call x1, Pallas kernels, local_fn(): pl.pallas_call(backward_kernel, name='backward', out_shape=(jax.ShapeDtyp...  122 us
    unnamed x8, local copies, waits for them, and re-layouts  9.46 us
    pallas_call x1, Pallas kernels, local_fn(): pl.pallas_call(lookup_kernel, name='lookup', out_shape=jax.ShapeDtypeStru...  6.28 us

profile of v2, /device:TPU:0, one launch (start us, length us, event | category | flops | bytes accessed | tf_op | source)
XLA Modules:
  0.0 265.2 jit_solution(17532522972128681782)
XLA Ops:
  0.6 123.1 %forward.1 = (bf16[64,1024]{1,0:T(8,128)(2,1)}, bf16[64,2048]{1,0:T(8,128)(2,1)}, bf16[8,1536,128]{2,1,0:T(8,128)(2,1)}, bf16[2048,8192]{1,0:T(8,128)(2,1)}) custom-call(s32[2048,8192]{1,0:T(8,128)} %mask.1, bf16[64,1024]{1,0:T(8,128)(2,1)} %bitcast.19, bf16[64,2048]{1,0:T(8,128)(2,1)} %bitcast.16), custom_call_target="tpu_custom_call" | custom-call | tf_op jit(solution)/shard_map/forward/pallas_call | solution.py:638
  123.8 0.7 dynamic-slice_bitcast_fusion
  124.5 0.1 fusion.2
  124.6 0.0 copy-start
  124.6 1.9 copy-done
  126.5 6.3 %lookup.1.g_in = f32[1032,128]{1,0:T(8,128)S(1)} custom-call(bf16[8,1536,128]{2,1,0:T(8,128)(2,1)S(1)} %copy-done, s32[1024]{0:T(1024)S(1)} %fusion.4.ru, s32[1024]{0:T(1024)S(1)} %bitcast.14, s32[1024]{0:T(1024)S(1)} %bitcast.13), custom_call_target="tpu_custom_call" | custom-call | tf_op jit(solution)/shard_map/lookup/pallas_call | solution.py:662
  132.8 0.0 copy-start.1
  132.8 0.8 copy-done.1
  133.6 1.8 fusion.9
  135.4 121.9 %backward.1 = (f32[64,1024]{1,0:T(8,128)}, f32[64,2048]{1,0:T(8,128)}, f32[8,128]{1,0:T(8,128)}) custom-call(bf16[2048,8192]{1,0:T(8,128)(2,1)} %get-tuple-element.14.a_hbm, f32[1032,128]{1,0:T(8,128)} %copy-done.1, s32[1,8192]{1,0:T(1,128)} %get-tuple-element.21.uid, s32[1,8192]{1,0:T(1,128)} %get-tuple-element.20.pid, s32[1,8192]{1,0:T(1,128)} %get-tuple-element.19.nid), custom_call_target="tpu_custom_call" | custom-call | tf_op jit(solution)/shard_map/backward/pallas_call | solution.py:672
  257.3 1.2 slice.33
  258.5 1.6 copy.13
  260.0 1.7 copy.14
  261.7 1.7 copy.15
  263.4 1.9 copy.16
  (3 shorter events, 0.0 us)
Async XLA Ops:
  124.6 1.9 copy-start
  132.8 0.8 copy-start.1

commit v3 on v2

--- a/solution.py
+++ b/solution.py
@@ -138,39 +138,50 @@
         own_u = lk.c * UB
         peer_u = (1 - lk.c) * UB
 
-        def far_cols(piece, half):
-            return _al(far + half * IB + piece * 1024, 128)
-
         if k > 0:
             for s in range(SX):
                 self.msg(FD, k - 1, s).wait_send()
                 self.msg(XR, k - 1, s).wait_send()
+                self.msg(FO, k - 1, s).wait_send()
                 self.msg(GF, k - 1, s).wait_send()
-
-        def far_own(j, _):
-            cols = pl.ds(_al(far + j * 1024, 128), 1024)
-            pi[:, cols] = _dot(eu[k, :, pl.ds(_al(own_u, 128), UB)], a[pl.ds(_al(own_u, 128), UB), cols])
-            return 0
-
-        lax.fori_loop(0, 4, far_own, 0)
+        own_rows = pl.ds(_al(own_u, 128), UB)
+        peer_rows = pl.ds(_al(peer_u, 128), UB)
+
+        def over_own(first_col):
+            def body(j, _):
+                cols = pl.ds(_al(first_col + j * 1024, 128), 1024)
+                pi[:, cols] = _dot(eu[k, :, own_rows], a[own_rows, cols])
+                return 0
+
+            lax.fori_loop(0, 4, body, 0)
+
+        over_own(far)
+        if between is not None:
+            between()
+        over_own(near)
         for s in range(SY):
             self.msg(YG, k, s).wait_recv()
 
-        def far_peer(j, _):
-            e = eu[k, :, pl.ds(_al(peer_u, 128), UB)]
-            rows = pl.ds(_al(peer_u, 128), UB)
-            first = j < 2
-            half = jnp.where(first, 1 - lk.h, lk.h)
+        def over_peer(j, _):
+            stage = j // 2
             p = j % 2
-            cols = pl.ds(far_cols(p, half), 1024)
-            pi[:, cols] = pi[:, cols] + _dot(e, a[rows, cols])
-
-            @pl.when(first)
+            is_far = 1 - stage % 2
+            mine = stage // 2
+            half = mine * lk.h + (1 - mine) * (1 - lk.h)
+            cols = pl.ds(_al(is_far * far + (1 - is_far) * near + half * IB + p * 1024, 128), 1024)
+            pi[:, cols] = pi[:, cols] + _dot(eu[k, :, peer_rows], a[peer_rows, cols])
+
+            @pl.when(stage == 0)
             def _():
                 for q in range(2):
                     self.msg(FD, k, 2 * p + q).start()
 
-            @pl.when(j >= 2)
+            @pl.when(stage == 1)
+            def _():
+                for q in range(2):
+                    self.msg(FO, k, 2 * p + q).start()
+
+            @pl.when(stage == 2)
             def _():
                 for q in range(2):
                     s = 2 * p + q
@@ -178,28 +189,14 @@
                     cs = pl.ds(_al(far + lk.h * IB + s * WX, 128), WX)
                     pi[:, cs] = pi[:, cs] + self.rf[k, :, pl.ds(_al(s * WX, 128), WX)]
                     self.msg(XR, k, s).start()
+
+            @pl.when(stage == 3)
+            def _():
+                self.msg(GX, k, p).wait_recv()
+                self.msg(GF, k, p).start()
             return 0
 
-        lax.fori_loop(0, 4, far_peer, 0)
-        if between is not None:
-            between()
-
-        if k > 0:
-            for s in range(SX):
-                self.msg(FO, k - 1, s).wait_send()
-
-        def near_items_t(s, _):
-            e = eu[k]
-            c1 = pl.ds(_al(near + (1 - lk.h) * IB + s * WX, 128), WX)
-            c2 = pl.ds(_al(near + lk.h * IB + s * WX, 128), WX)
-            pi[:, c1] = _dot(e, a[:, c1])
-            self.msg(FO, k, s).start()
-            pi[:, c2] = _dot(e, a[:, c2])
-            self.msg(GX, k, s).wait_recv()
-            self.msg(GF, k, s).start()
-            return 0
-
-        lax.fori_loop(0, SX, near_items_t, 0)
+        lax.fori_loop(0, 8, over_peer, 0)
 
         if k > 0:
             for s in range(SY):
@@ -220,10 +217,10 @@
             user_final(k, s, pu[:, uc] + self.ry[k, :, s * WY:(s + 1) * WY])
 
         def users_tile(t, _):
-            u = t // 2
-            is_far = t % 2
-            own = u // 2
-            base = own * own_u + (1 - own) * peer_u + (u % 2) * WY
+            own = t // 4
+            u = own * ((t // 2) % 2) + (1 - own) * (t % 2)
+            is_far = own * (t % 2) + (1 - own) * ((t // 2) % 2)
+            base = own * own_u + (1 - own) * peer_u + u * WY
             at = is_far * far + (1 - is_far) * near
             rows = pl.ds(_al(base, 512), WY)
             uc = pl.ds(_al(base, 128), WY)
@@ -234,38 +231,40 @@
             def _():
                 pu[:, uc] = v
 
+            @pl.when(is_far == 1)
+            def _():
+                pu[:, uc] = pu[:, uc] + v
+
             @pl.when(t == 0)
+            def _():
+                for s in range(2, SX):
+                    self.msg(GX, k, s).wait_recv()
+                    self.msg(GF, k, s).start()
+
+            @pl.when(t == 1)
             def _():
                 for s in range(SX):
                     self.msg(GF, k, s).wait_recv()
 
-            @pl.when(is_far == 1)
-            def _():
-                pu[:, uc] = pu[:, uc] + v
-
-            @pl.when(t == 1)
-            def _():
-                self.msg(YR, k, 0).start()
-
-            @pl.when(t == 2)
+            @pl.when((t == 2) | (t == 3))
+            def _():
+                self.msg(YR, k, t - 2).start()
+
+            @pl.when(t == 3)
             def _():
                 item_piece(0)
 
-            @pl.when(t == 3)
-            def _():
-                self.msg(YR, k, 1).start()
-
-            @pl.when(t == 4)
+            @pl.when(t == 5)
             def _():
                 item_piece(1)
 
             @pl.when(t == 6)
             def _():
                 user_piece(0)
-                item_piece(2)
             return 0
 
         lax.fori_loop(0, 8, users_tile, 0)
+        item_piece(2)
         user_piece(1)
         item_piece(3)
 

time: 266 us -> 260 us (0.977)
  Pallas kernels: 251 us -> 245 us
    pallas_call x1, Pallas kernels: 122 us -> 118 us  [local_fn(): pl.pallas_call(backward_kernel, name='backward', out_shape=(jax.ShapeDtyp...]
where the time goes in v3:
time: 260 us; the launch traced here: 259 us
  Pallas kernels  245 us (94%)
  local copies, waits for them, and re-layouts  13.2 us (5%)
    pallas_call x1, Pallas kernels, local_fn(): pl.pallas_call(forward_kernel, name='forward', out_shape=(jax.ShapeDtypeS...  121 us
    pallas_call x1, Pallas kernels, local_fn(): pl.pallas_call(backward_kernel, name='backward', out_shape=(jax.ShapeDtyp...  118 us
    unnamed x8, local copies, waits for them, and re-layouts  9.46 us
    pallas_call x1, Pallas kernels, local_fn(): pl.pallas_call(lookup_kernel, name='lookup', out_shape=jax.ShapeDtypeStru...  6.28 us

profile of v3, /device:TPU:0, one launch (start us, length us, event | category | flops | bytes accessed | tf_op | source)
XLA Modules:
  0.0 259.3 jit_solution(11494551066761044808)
XLA Ops:
  0.6 121.1 %forward.1 = (bf16[64,1024]{1,0:T(8,128)(2,1)}, bf16[64,2048]{1,0:T(8,128)(2,1)}, bf16[8,1536,128]{2,1,0:T(8,128)(2,1)}, bf16[2048,8192]{1,0:T(8,128)(2,1)}) custom-call(s32[2048,8192]{1,0:T(8,128)} %mask.1, bf16[64,1024]{1,0:T(8,128)(2,1)} %bitcast.19, bf16[64,2048]{1,0:T(8,128)(2,1)} %bitcast.16), custom_call_target="tpu_custom_call" | custom-call | tf_op jit(solution)/shard_map/forward/pallas_call | solution.py:637
  121.8 0.7 dynamic-slice_bitcast_fusion
  122.5 0.1 fusion.2
  122.6 0.0 copy-start
  122.6 1.9 copy-done
  124.5 6.3 %lookup.1.g_in = f32[1032,128]{1,0:T(8,128)S(1)} custom-call(bf16[8,1536,128]{2,1,0:T(8,128)(2,1)S(1)} %copy-done, s32[1024]{0:T(1024)S(1)} %fusion.4.ru, s32[1024]{0:T(1024)S(1)} %bitcast.14, s32[1024]{0:T(1024)S(1)} %bitcast.13), custom_call_target="tpu_custom_call" | custom-call | tf_op jit(solution)/shard_map/lookup/pallas_call | solution.py:661
  130.8 0.0 copy-start.1
  130.8 0.8 copy-done.1
  131.6 1.8 fusion.9
  133.4 117.9 %backward.1 = (f32[64,1024]{1,0:T(8,128)}, f32[64,2048]{1,0:T(8,128)}, f32[8,128]{1,0:T(8,128)}) custom-call(bf16[2048,8192]{1,0:T(8,128)(2,1)} %get-tuple-element.14.a_hbm, f32[1032,128]{1,0:T(8,128)} %copy-done.1, s32[1,8192]{1,0:T(1,128)} %get-tuple-element.21.uid, s32[1,8192]{1,0:T(1,128)} %get-tuple-element.20.pid, s32[1,8192]{1,0:T(1,128)} %get-tuple-element.19.nid), custom_call_target="tpu_custom_call" | custom-call | tf_op jit(solution)/shard_map/backward/pallas_call | solution.py:671
  251.3 1.2 slice.33
  252.5 1.6 copy.13
  254.1 1.7 copy.14
  255.8 1.7 copy.15
  257.4 1.9 copy.16
  (3 shorter events, 0.0 us)
Async XLA Ops:
  122.6 1.9 copy-start
  130.8 0.8 copy-start.1

commit v4 on v3

--- a/solution.py
+++ b/solution.py
@@ -148,12 +148,8 @@
         peer_rows = pl.ds(_al(peer_u, 128), UB)
 
         def over_own(first_col):
-            def body(j, _):
-                cols = pl.ds(_al(first_col + j * 1024, 128), 1024)
-                pi[:, cols] = _dot(eu[k, :, own_rows], a[own_rows, cols])
-                return 0
-
-            lax.fori_loop(0, 4, body, 0)
+            cols = pl.ds(_al(first_col, 128), 2 * IB)
+            pi[:, cols] = _dot(eu[k, :, own_rows], a[own_rows, cols])
 
         over_own(far)
         if between is not None:
@@ -162,41 +158,39 @@
         for s in range(SY):
             self.msg(YG, k, s).wait_recv()
 
-        def over_peer(j, _):
-            stage = j // 2
-            p = j % 2
+        def over_peer(stage, _):
             is_far = 1 - stage % 2
             mine = stage // 2
             half = mine * lk.h + (1 - mine) * (1 - lk.h)
-            cols = pl.ds(_al(is_far * far + (1 - is_far) * near + half * IB + p * 1024, 128), 1024)
+            cols = pl.ds(_al(is_far * far + (1 - is_far) * near + half * IB, 128), IB)
             pi[:, cols] = pi[:, cols] + _dot(eu[k, :, peer_rows], a[peer_rows, cols])
 
             @pl.when(stage == 0)
             def _():
-                for q in range(2):
-                    self.msg(FD, k, 2 * p + q).start()
+                for s in range(SX):
+                    self.msg(FD, k, s).start()
 
             @pl.when(stage == 1)
             def _():
-                for q in range(2):
-                    self.msg(FO, k, 2 * p + q).start()
+                for s in range(SX):
+                    self.msg(FO, k, s).start()
 
             @pl.when(stage == 2)
             def _():
-                for q in range(2):
-                    s = 2 * p + q
+                for s in range(SX):
                     self.msg(FD, k, s).wait_recv()
                     cs = pl.ds(_al(far + lk.h * IB + s * WX, 128), WX)
-                    pi[:, cs] = pi[:, cs] + self.rf[k, :, pl.ds(_al(s * WX, 128), WX)]
+                    pi[:, cs] = pi[:, cs] + self.rf[k, :, s * WX:(s + 1) * WX]
                     self.msg(XR, k, s).start()
 
             @pl.when(stage == 3)
             def _():
-                self.msg(GX, k, p).wait_recv()
-                self.msg(GF, k, p).start()
+                for s in range(2):
+                    self.msg(GX, k, s).wait_recv()
+                    self.msg(GF, k, s).start()
             return 0
 
-        lax.fori_loop(0, 8, over_peer, 0)
+        lax.fori_loop(0, 4, over_peer, 0)
 
         if k > 0:
             for s in range(SY):
@@ -281,41 +275,47 @@
 
 
 class AllGather:
-    def __init__(self, lk, ref, rows, ss, rs):
-        self.lk, self.ref, self.rows, self.ss, self.rs = lk, ref, rows, ss, rs
+    def __init__(self, lk, ref, start, n_lo, n_hi, ss, rs):
+        self.lk, self.ref, self.ss, self.rs = lk, ref, ss, rs
+        self.full, self.lo, self.hi = pl.ds(start, n_lo + n_hi), pl.ds(start, n_lo), pl.ds(start + n_lo, n_hi)
+        self.two = n_hi > 0
 
     def _copy(self, i):
         lk = self.lk
-        own = lk.slot
         xs, ys, ds_ = _slot_of(lk.xn), _slot_of(lk.yn), _slot_of(lk.diag)
-        src_slot = (own, own, own, own, xs, ys, ds_)[i]
-        dev = (lk.partner, lk.xn, lk.yn, lk.diag, lk.partner, lk.partner, lk.partner)[i]
-        ref = self.ref.at[src_slot, self.rows]
+        src_slot = (lk.slot, lk.slot, lk.slot, xs, ys, xs, ys, ds_, ds_)[i]
+        dev = (lk.partner, lk.xn, lk.yn, lk.yn, lk.xn, lk.partner, lk.partner, lk.partner, lk.partner)[i]
+        rows = (self.full, self.full, self.full, self.lo, self.hi, self.full, self.full, self.lo, self.hi)[i]
+        ref = self.ref.at[src_slot, rows]
         return _remote(ref, ref, self.ss.at[i], self.rs.at[i], dev)
 
+    def _used(self, i):
+        return self.two or i not in (4, 8)
+
     def start(self):
-        for i in (1, 2, 0, 3):
+        for i in (1, 2, 0):
             self._copy(i).start()
 
     def arrive(self, i):
+        if not self._used(i):
+            return
         self._copy(i).wait_recv()
-        if i in (1, 2, 3):
-            self._copy(i + 3).start()
+        for j in {1: (3, 5), 2: (4, 6), 3: (7,), 4: (8,)}.get(i, ()):
+            if self._used(j):
+                self._copy(j).start()
 
     def slot(self, i):
         lk = self.lk
         c, x, h = lk.c, lk.x, lk.h
-        row = (2 * x + 1 - h, 2 * (1 - x) + h, lk.r, 2 * (1 - x) + h,
-               2 * (1 - x) + 1 - h, 2 * x + 1 - h, 2 * (1 - x) + 1 - h)[i]
-        col = (c, c, 1 - c, 1 - c, c, 1 - c, 1 - c)[i]
+        row = {0: 2 * x + 1 - h, 1: 2 * (1 - x) + h, 2: lk.r, 4: 2 * (1 - x) + h,
+               5: 2 * (1 - x) + 1 - h, 6: 2 * x + 1 - h, 8: 2 * (1 - x) + 1 - h}[i]
+        col = {0: c, 1: c, 2: 1 - c, 4: 1 - c, 5: c, 6: 1 - c, 8: 1 - c}[i]
         return row * 2 + col
 
     def drain(self):
-        for i in range(7):
-            self._copy(i).wait_send()
-
-
-ORDER = (0, 1, 2, 4, 5, 3, 6)
+        for i in range(9):
+            if self._used(i):
+                self._copy(i).wait_send()
 
 
 def _unpack_t(xt):
@@ -345,7 +345,7 @@
 
 def forward_kernel(mask, e0u, e0i, out_u, out_i, table, a_hbm,
                    a, ei, eu, pi, pu, rf, ro, rx, ry, ss, rs,
-                   mbuf, msem, csum, rpart, dcol, drow, dss, drs, su, si, uacc, iacc, asem, tss, trs, iss, irs):
+                   mbuf, msem, csum, rpart, dcol, drow, dss, drs, su, si, uacc, iacc, asem, iss, irs):
     lk = Links()
 
     def mask_copy(j):
@@ -449,31 +449,33 @@
         if k < STEPS - 1:
             pr.put_item(k + 1, s, b)
         iacc[:, s * WX:(s + 1) * WX] = iacc[:, s * WX:(s + 1) * WX] + b.astype(F32)
-        if k == STEPS - 1 and s == SX - 1:
-            t = iacc[...] * 0.25
-            table[lk.slot, PU:PR, :] = _unpack_t(t).astype(BF16)
-            ag_i.start()
-            out_i[...] = t.astype(BF16)
-
-    ag_u = AllGather(lk, table, pl.ds(0, PU), tss, trs)
-    ag_i = AllGather(lk, table, pl.ds(PU, PI), iss, irs)
+        if k == STEPS - 1:
+            t = iacc[:, s * WX:(s + 1) * WX] * 0.25
+            table[lk.slot, PU + s * WX // 2:PU + (s + 1) * WX // 2, :] = _unpack_t(t).astype(BF16)
+            ags[s].start()
+            out_i[:, s * WX:(s + 1) * WX] = t.astype(BF16)
+
+    ags = [AllGather(lk, table, PU + s * WX // 2, WX // 2, 0, iss.at[s], irs.at[s]) for s in range(SX)]
+    ag_u = AllGather(lk, table, 0, PU, 0, iss.at[SX], irs.at[SX])
+    ags.append(ag_u)
     for k in range(STEPS):
         pr.step(k, user_final, item_final, scale_near if k == 0 else None)
-    for ag in (ag_u, ag_i):
-        for i in ORDER:
-            ag.arrive(i)
+    for group in ((1, 2), (3,), (0, 5, 6, 7)):
+        for s in (SX, 0, 1, 2, 3):
+            for i in group:
+                ags[s].arrive(i)
     for cp in dcopies:
         cp.wait_send()
     for j in range(AW):
         a_copy(j).wait()
     pr.finish()
-    ag_u.drain()
-    ag_i.drain()
+    for ag in ags:
+        ag.drain()
 
 
 def lookup_kernel(table, ru, rp, rn, out, tab, gu, gp, gn):
     def unpack(b, _):
-        for lo, n, dst in ((0, PU, 0), (PU, PI, UB)):
+        for lo, n, dst in [(0, PU, 0)] + [(PU + s * WX // 2, WX // 2, UB + s * WX) for s in range(SX)]:
             for o in range(0, n, 128):
                 v = table[b, lo + o:lo + o + 128, :].astype(F32)
                 base = b * (UB + IB) + dst + o
@@ -521,7 +523,7 @@
     lk.barrier()
     pr = Prop(lk, a, ei, eu, pi, pu, rf, ro, rx, ry, ss, rs)
     gcopy.wait()
-    ag = AllGather(lk, g_all, pl.ds(0, TB + 8), gss, grs)
+    ag = AllGather(lk, g_all, 0, TB // 2, TB // 2 + 8, gss, grs)
     ag.start()
     acc_u[...] = jnp.zeros_like(acc_u)
     acc_i[...] = jnp.zeros_like(acc_i)
@@ -530,8 +532,8 @@
 
     def scatter(b):
         def split(m, _):
-            rows = pl.ds(_al(m * 128, 128), 128)
-            left = lax.broadcasted_iota(jnp.int32, (128, 128), 1) < D
+            rows = pl.ds(_al(m * 256, 256), 256)
+            left = lax.broadcasted_iota(jnp.int32, (256, 128), 1) < D
             g = g_all[b, rows, :]
             hi = g.astype(BF16).astype(F32)
             r1 = g - hi
@@ -543,7 +545,7 @@
             wi[rows, 128:256] = pltpu.roll(lo, D, 1).astype(BF16)
             return 0
 
-        lax.fori_loop(0, TB // 128, split, 0)
+        lax.fori_loop(0, TB // 256, split, 0)
         cols = pl.ds(_al(b * TB, 128), TB)
         sub = lax.broadcasted_iota(jnp.int32, (256, TB), 0).astype(F32).astype(BF16)
         one, zero = jnp.array(1.0, BF16), jnp.array(0.0, BF16)
@@ -553,26 +555,23 @@
             v = jnp.where((v >= 0) & (v < 256), v, -1).astype(F32)
             return jnp.broadcast_to(v, (256, TB)).astype(BF16)
 
-        def users(m, _):
-            hot = jnp.where(lanes(uid, base_u + m * 256) == sub, one, zero)
-            rows = pl.ds(_al(m * 256, 256), 256)
-            acc_u[rows, :] = acc_u[rows, :] + _dot(hot, wu[...])
+        def hot(ids, base):
+            return jnp.concatenate([jnp.where(lanes(ids, base + m * 256) == sub, one, zero) for m in range(4)], axis=0)
+
+        acc_u[...] = acc_u[...] + _dot(hot(uid, base_u), wu[...])
+
+        def items(m, _):
+            rows = pl.ds(_al(m * 1024, 1024), 1024)
+            acc_i[rows, :] = acc_i[rows, :] + _dot(hot(pid, base_i + m * 1024) - hot(nid, base_i + m * 1024), wi[...])
             return 0
 
-        def items(m, _):
-            hot_p = jnp.where(lanes(pid, base_i + m * 256) == sub, one, zero)
-            hot = hot_p - jnp.where(lanes(nid, base_i + m * 256) == sub, one, zero)
-            rows = pl.ds(_al(m * 256, 256), 256)
-            acc_i[rows, :] = acc_i[rows, :] + _dot(hot, wi[...])
-            return 0
-
-        lax.fori_loop(0, UB // 256, users, 0)
-        lax.fori_loop(0, IB // 256, items, 0)
+        lax.fori_loop(0, IB // 1024, items, 0)
 
     scatter(lk.slot)
-    for i in ORDER:
-        ag.arrive(i)
-        scatter(ag.slot(i))
+    for group in ((0,), (1,), (2,), (5,), (6,), (3, 4), (7, 8)):
+        for i in group:
+            ag.arrive(i)
+        scatter(ag.slot(group[-1]))
 
     loss = g_all[0, TB:TB + 8, :]
     for b in range(1, 8):
@@ -618,6 +617,11 @@
         pr.step(k, user_final, item_final)
     pr.finish()
     ag.drain()
+
+
+def finish_kernel(*refs):
+    for src, dst in zip(refs[:4], refs[4:]):
+        dst[...] = src[...]
 
 
 VM = pl.BlockSpec(memory_space=pltpu.VMEM)
@@ -647,7 +651,7 @@
                 pltpu.VMEM((4, 8, 1024), F32), pltpu.VMEM((2, 8, RU), F32), DMA((4,)), DMA((4,)),
                 pltpu.VMEM((RU, 128), F32), pltpu.VMEM((1, CI), F32),
                 pltpu.VMEM((D, UB), F32), pltpu.VMEM((D, IB), F32), DMA((AW,)),
-                DMA((7,)), DMA((7,)), DMA((7,)), DMA((7,)),
+                DMA((SX + 1, 9)), DMA((SX + 1, 9)),
             ],
             compiler_params=_params(0),
         )(mask, e0u.T, e0i.T)
@@ -676,13 +680,21 @@
             in_specs=[ANY, ANY, VM, VM, VM],
             out_specs=(VM, VM, VM),
             scratch_shapes=PROP_SCRATCH + [
-                DMA, pltpu.VMEM((8, TB + 8, 128), F32), DMA, DMA((7,)), DMA((7,)),
+                DMA, pltpu.VMEM((8, TB + 8, 128), F32), DMA, DMA((9,)), DMA((9,)),
                 pltpu.VMEM((TB, 256), BF16), pltpu.VMEM((TB, 256), BF16),
                 pltpu.VMEM((UB, 256), F32), pltpu.VMEM((IB, 256), F32),
                 pltpu.VMEM((D, UB), F32), pltpu.VMEM((D, IB), F32),
             ],
             compiler_params=_params(1),
         )(a_hbm, g, cols[0:1], cols[1:2], cols[2:3])
+        outs = (out_u, out_i, d_u, d_i)
+        out_u, out_i, d_u, d_i = pl.pallas_call(
+            finish_kernel,
+            name='finish',
+            out_shape=tuple(jax.ShapeDtypeStruct(o.shape, o.dtype) for o in outs),
+            in_specs=[VM] * 4,
+            out_specs=(VM,) * 4,
+        )(*outs)
         return out_u.T, out_i.T, loss[0, 0], d_u.T, d_i.T
 
     user_spec = P(('row', 'col'), None)

time: 260 us -> 237 us (0.912)
  Pallas kernels: 245 us -> 229 us
  local copies, waits for them, and re-layouts: 13.2 us -> 6.37 us
    pallas_call x1, Pallas kernels: 118 us -> 105 us  [local_fn(): pl.pallas_call(backward_kernel, name='backward', out_shape=(jax.ShapeDtyp...]
    unnamed x8 -> x4, local copies, waits for them, and re-layouts: 9.46 us -> 2.68 us
    pallas_call x1, Pallas kernels: 121 us -> 116 us  [local_fn(): pl.pallas_call(forward_kernel, name='forward', out_shape=(jax.ShapeDtypeS...]
where the time goes in v4:
time: 237 us; the launch traced here: 236 us
  Pallas kernels  229 us (97%)
  local copies, waits for them, and re-layouts  6.37 us (3%)
    pallas_call x1, Pallas kernels, local_fn(): pl.pallas_call(forward_kernel, name='forward', out_shape=(jax.ShapeDtypeS...  116 us
    pallas_call x1, Pallas kernels, local_fn(): pl.pallas_call(backward_kernel, name='backward', out_shape=(jax.ShapeDtyp...  105 us
    pallas_call x1, Pallas kernels, local_fn(): pl.pallas_call(lookup_kernel, name='lookup', out_shape=jax.ShapeDtypeStru...  6.46 us

profile of v4, /device:TPU:0, one launch (start us, length us, event | category | flops | bytes accessed | tf_op | source)
XLA Modules:
  0.0 236.4 jit_solution(10301664870686699222)
XLA Ops:
  0.6 116.0 %forward.1 = (bf16[64,1024]{1,0:T(8,128)(2,1)}, bf16[64,2048]{1,0:T(8,128)(2,1)}, bf16[8,1536,128]{2,1,0:T(8,128)(2,1)}, bf16[2048,8192]{1,0:T(8,128)(2,1)}) custom-call(s32[2048,8192]{1,0:T(8,128)} %mask.1, bf16[64,1024]{1,0:T(8,128)(2,1)} %bitcast.16, bf16[64,2048]{1,0:T(8,128)(2,1)} %bitcast.15), custom_call_target="tpu_custom_call" | custom-call | tf_op jit(solution)/shard_map/forward/pallas_call | solution.py:641
  116.6 0.7 dynamic-slice_bitcast_fusion
  117.4 0.1 fusion.2
  117.4 0.0 copy-start
  117.5 1.9 copy-done
  119.3 6.5 %lookup.1.g_in = f32[1032,128]{1,0:T(8,128)S(1)} custom-call(bf16[8,1536,128]{2,1,0:T(8,128)(2,1)S(1)} %copy-done, s32[1024]{0:T(1024)S(1)} %fusion.4.ru, s32[1024]{0:T(1024)S(1)} %bitcast.14, s32[1024]{0:T(1024)S(1)} %bitcast.13), custom_call_target="tpu_custom_call" | custom-call | tf_op jit(solution)/shard_map/lookup/pallas_call | solution.py:665
  125.8 0.0 copy-start.1
  125.8 0.8 copy-done.1
  126.6 1.8 fusion.9
  128.4 104.5 %backward.1 = (f32[64,1024]{1,0:T(8,128)}, f32[64,2048]{1,0:T(8,128)}, f32[8,128]{1,0:T(8,128)}) custom-call(bf16[2048,8192]{1,0:T(8,128)(2,1)} %get-tuple-element.18.a_hbm, f32[1032,128]{1,0:T(8,128)} %copy-done.1, s32[1,8192]{1,0:T(1,128)} %get-tuple-element.29.uid, s32[1,8192]{1,0:T(1,128)} %get-tuple-element.28.pid, s32[1,8192]{1,0:T(1,128)} %get-tuple-element.27.nid), custom_call_target="tpu_custom_call" | custom-call | tf_op jit(solution)/shard_map/backward/pallas_call | solution.py:675
  232.9 2.3 finish.1
  235.2 1.2 slice.33
  (3 shorter events, 0.0 us)
Async XLA Ops:
  117.4 1.9 copy-start
  125.8 0.8 copy-start.1

commit v5 on v4

--- a/solution.py
+++ b/solution.py
@@ -147,35 +147,34 @@
         own_rows = pl.ds(_al(own_u, 128), UB)
         peer_rows = pl.ds(_al(peer_u, 128), UB)
 
-        def over_own(first_col):
-            cols = pl.ds(_al(first_col, 128), 2 * IB)
+        def over_own(j, _):
+            cols = pl.ds(_al(far + j * (near - far), 128), 2 * IB)
             pi[:, cols] = _dot(eu[k, :, own_rows], a[own_rows, cols])
-
-        over_own(far)
-        if between is not None:
-            between()
-        over_own(near)
+            return 0
+
+        late_near = between is not None
+        lax.fori_loop(0, 1 if late_near else 2, over_own, 0)
         for s in range(SY):
             self.msg(YG, k, s).wait_recv()
 
         def over_peer(stage, _):
-            is_far = 1 - stage % 2
-            mine = stage // 2
+            is_far = 1 - (stage // 2 if late_near else stage % 2)
+            mine = stage % 2 if late_near else stage // 2
             half = mine * lk.h + (1 - mine) * (1 - lk.h)
             cols = pl.ds(_al(is_far * far + (1 - is_far) * near + half * IB, 128), IB)
             pi[:, cols] = pi[:, cols] + _dot(eu[k, :, peer_rows], a[peer_rows, cols])
 
-            @pl.when(stage == 0)
+            @pl.when(is_far * (1 - mine) == 1)
             def _():
                 for s in range(SX):
                     self.msg(FD, k, s).start()
 
-            @pl.when(stage == 1)
+            @pl.when((1 - is_far) * (1 - mine) == 1)
             def _():
                 for s in range(SX):
                     self.msg(FO, k, s).start()
 
-            @pl.when(stage == 2)
+            @pl.when(is_far * mine == 1)
             def _():
                 for s in range(SX):
                     self.msg(FD, k, s).wait_recv()
@@ -183,14 +182,20 @@
                     pi[:, cs] = pi[:, cs] + self.rf[k, :, s * WX:(s + 1) * WX]
                     self.msg(XR, k, s).start()
 
-            @pl.when(stage == 3)
+            @pl.when((1 - is_far) * mine == 1)
             def _():
                 for s in range(2):
                     self.msg(GX, k, s).wait_recv()
                     self.msg(GF, k, s).start()
             return 0
 
-        lax.fori_loop(0, 4, over_peer, 0)
+        if late_near:
+            lax.fori_loop(0, 2, over_peer, 0)
+            between()
+            lax.fori_loop(1, 2, over_own, 0)
+            lax.fori_loop(2, 4, over_peer, 0)
+        else:
+            lax.fori_loop(0, 4, over_peer, 0)
 
         if k > 0:
             for s in range(SY):
@@ -473,8 +478,15 @@
         ag.drain()
 
 
-def lookup_kernel(table, ru, rp, rn, out, tab, gu, gp, gn):
+def lookup_kernel(table_hbm, ids, out, table, tsem, tab, gu, gp, gn):
+    def load(b):
+        return pltpu.make_async_copy(table_hbm.at[b], table.at[b], tsem.at[b])
+
+    for b in range(8):
+        load(b).start()
+
     def unpack(b, _):
+        load(b).wait()
         for lo, n, dst in [(0, PU, 0)] + [(PU + s * WX // 2, WX // 2, UB + s * WX) for s in range(SX)]:
             for o in range(0, n, 128):
                 v = table[b, lo + o:lo + o + 128, :].astype(F32)
@@ -488,9 +500,9 @@
     def gather(g, _):
         for o in range(8):
             t = g * 8 + o
-            gu[pl.ds(t, 1), :] = tab[pl.ds(ru[t], 1), :]
-            gp[pl.ds(t, 1), :] = tab[pl.ds(rp[t], 1), :]
-            gn[pl.ds(t, 1), :] = tab[pl.ds(rn[t], 1), :]
+            gu[pl.ds(t, 1), :] = tab[pl.ds(ids[0, t], 1), :]
+            gp[pl.ds(t, 1), :] = tab[pl.ds(ids[1, t], 1), :]
+            gn[pl.ds(t, 1), :] = tab[pl.ds(ids[2, t], 1), :]
         return 0
 
     lax.fori_loop(0, TB // 8, gather, 0)
@@ -512,7 +524,7 @@
     out[TB:TB + 8, :] = jnp.broadcast_to(tot, (8, 128))
 
 
-def backward_kernel(a_hbm, g_in, uid, pid, nid, out_u, out_i, out_l,
+def backward_kernel(a_hbm, g_in, ids, out_u, out_i, out_l,
                     a, ei, eu, pi, pu, rf, ro, rx, ry, ss, rs,
                     asem, g_all, gsem, gss, grs, wu, wi, acc_u, acc_i, su, si):
     lk = Links()
@@ -550,19 +562,19 @@
         sub = lax.broadcasted_iota(jnp.int32, (256, TB), 0).astype(F32).astype(BF16)
         one, zero = jnp.array(1.0, BF16), jnp.array(0.0, BF16)
 
-        def lanes(ids, base):
-            v = ids[:, cols] - base
+        def lanes(which, base):
+            v = ids[which:which + 1, cols] - base
             v = jnp.where((v >= 0) & (v < 256), v, -1).astype(F32)
             return jnp.broadcast_to(v, (256, TB)).astype(BF16)
 
-        def hot(ids, base):
-            return jnp.concatenate([jnp.where(lanes(ids, base + m * 256) == sub, one, zero) for m in range(4)], axis=0)
-
-        acc_u[...] = acc_u[...] + _dot(hot(uid, base_u), wu[...])
+        def hot(which, base):
+            return jnp.concatenate([jnp.where(lanes(which, base + m * 256) == sub, one, zero) for m in range(4)], axis=0)
+
+        acc_u[...] = acc_u[...] + _dot(hot(0, base_u), wu[...])
 
         def items(m, _):
             rows = pl.ds(_al(m * 1024, 1024), 1024)
-            acc_i[rows, :] = acc_i[rows, :] + _dot(hot(pid, base_i + m * 1024) - hot(nid, base_i + m * 1024), wi[...])
+            acc_i[rows, :] = acc_i[rows, :] + _dot(hot(1, base_i + m * 1024) - hot(2, base_i + m * 1024), wi[...])
             return 0
 
         lax.fori_loop(0, IB // 1024, items, 0)
@@ -659,25 +671,26 @@
         cols = triples.T
         mine = lax.dynamic_slice(cols, (0, slot * TB), (3, TB))
         per = UB + IB
-        row_u = (mine[0] // UB) * per + mine[0] % UB
-        blk = mine[1:] // IB
-        row_i = ((blk % 4) * 2 + blk // 4) * per + UB + mine[1:] % IB
+        blk = mine // IB
+        row_i = ((blk % 4) * 2 + blk // 4) * per + UB + mine % IB
+        row_u = (mine // UB) * per + mine % UB
+        ids = jnp.where(lax.broadcasted_iota(jnp.int32, (3, TB), 0) == 0, row_u, row_i)
         g = pl.pallas_call(
             lookup_kernel,
             name='lookup',
             out_shape=jax.ShapeDtypeStruct((TB + 8, 128), F32),
-            in_specs=[VM, SM, SM, SM],
+            in_specs=[ANY, SM],
             out_specs=VM,
-            scratch_shapes=[pltpu.VMEM((8 * per, 128), F32)] + [pltpu.VMEM((TB, 128), F32)] * 3,
-            compiler_params=pltpu.CompilerParams(vmem_limit_bytes=40 * 1024 * 1024),
-        )(table, row_u, row_i[0], row_i[1])
+            scratch_shapes=[pltpu.VMEM((8, PR, 128), BF16), DMA((8,)), pltpu.VMEM((8 * per, 128), F32)] + [pltpu.VMEM((TB, 128), F32)] * 3,
+            compiler_params=pltpu.CompilerParams(vmem_limit_bytes=VMEM_LIMIT),
+        )(table, ids)
 
         d_u, d_i, loss = pl.pallas_call(
             backward_kernel,
             name='backward',
             out_shape=(jax.ShapeDtypeStruct((D, UB), F32), jax.ShapeDtypeStruct((D, IB), F32),
                        jax.ShapeDtypeStruct((8, 128), F32)),
-            in_specs=[ANY, ANY, VM, VM, VM],
+            in_specs=[ANY, ANY, VM],
             out_specs=(VM, VM, VM),
             scratch_shapes=PROP_SCRATCH + [
                 DMA, pltpu.VMEM((8, TB + 8, 128), F32), DMA, DMA((9,)), DMA((9,)),
@@ -686,7 +699,7 @@
                 pltpu.VMEM((D, UB), F32), pltpu.VMEM((D, IB), F32),
             ],
             compiler_params=_params(1),
-        )(a_hbm, g, cols[0:1], cols[1:2], cols[2:3])
+        )(a_hbm, g, cols)
         outs = (out_u, out_i, d_u, d_i)
         out_u, out_i, d_u, d_i = pl.pallas_call(
             finish_kernel,

time: 237 us -> 237 us (level)
  local copies, waits for them, and re-layouts: 6.37 us -> 1.19 us
  Pallas kernels: 229 us -> 234 us
    pallas_call x1, Pallas kernels: 6.46 us -> 10.7 us  [local_fn(): pl.pallas_call(lookup_kernel, name='lookup', out_shape=jax.ShapeDtypeStru...]
    unnamed x4 -> x0, local copies, waits for them, and re-layouts: 2.68 us -> none
where the time goes in v5:
time: 237 us
  Pallas kernels  234 us (99%)
    pallas_call x1, Pallas kernels, local_fn(): pl.pallas_call(forward_kernel, name='forward', out_shape=(jax.ShapeDtypeS...  116 us
    pallas_call x1, Pallas kernels, local_fn(): pl.pallas_call(backward_kernel, name='backward', out_shape=(jax.ShapeDtyp...  104 us
    pallas_call x1, Pallas kernels, local_fn(): pl.pallas_call(lookup_kernel, name='lookup', out_shape=jax.ShapeDtypeStru...  10.7 us

profile of v5, /device:TPU:0, one launch (start us, length us, event | category | flops | bytes accessed | tf_op | source)
XLA Modules:
  0.0 237.2 jit_solution(16521280073217490799)
XLA Ops:
  0.6 1.4 fusion.2.ids
  2.1 116.5 %forward.1 = (bf16[64,1024]{1,0:T(8,128)(2,1)}, bf16[64,2048]{1,0:T(8,128)(2,1)}, bf16[8,1536,128]{2,1,0:T(8,128)(2,1)}, bf16[2048,8192]{1,0:T(8,128)(2,1)}) custom-call(s32[2048,8192]{1,0:T(8,128)} %mask.1, bf16[64,1024]{1,0:T(8,128)(2,1)} %bitcast.22, bf16[64,2048]{1,0:T(8,128)(2,1)} %bitcast.20), custom_call_target="tpu_custom_call" | custom-call | tf_op jit(solution)/shard_map/forward/pallas_call | solution.py:653
  118.6 10.7 %lookup.1.g_in = f32[1032,128]{1,0:T(8,128)} custom-call(bf16[8,1536,128]{2,1,0:T(8,128)(2,1)} %get-tuple-element.19.table_hbm, s32[3,1024]{1,0:T(4,128)} %fusion.2.ids), custom_call_target="tpu_custom_call" | custom-call | tf_op jit(solution)/shard_map/lookup/pallas_call | solution.py:678
  129.3 104.4 %backward.1 = (f32[64,1024]{1,0:T(8,128)}, f32[64,2048]{1,0:T(8,128)}, f32[8,128]{1,0:T(8,128)}) custom-call(bf16[2048,8192]{1,0:T(8,128)(2,1)} %get-tuple-element.18.a_hbm, f32[1032,128]{1,0:T(8,128)} %lookup.1.g_in, s32[3,8192]{1,0:T(4,128)} %bitcast.21), custom_call_target="tpu_custom_call" | custom-call | tf_op jit(solution)/shard_map/backward/pallas_call | solution.py:688
  233.7 1.2 slice.3
  234.9 2.3 finish.1
  (1 shorter events, 0.0 us)

commit v6 on v5

--- a/solution.py
+++ b/solution.py
@@ -82,6 +82,7 @@
         self.a, self.ei, self.eu, self.pi, self.pu = a, ei, eu, pi, pu
         self.rf, self.ro, self.rx, self.ry = rf, ro, rx, ry
         self.ss, self.rs = ss, rs
+        pu[...] = jnp.zeros_like(pu)
 
     def msg(self, kind, k, s):
         lk = self.lk
@@ -225,14 +226,7 @@
             uc = pl.ds(_al(base, 128), WY)
             cols = pl.ds(_al(at, 128), 2 * IB)
             v = _dot_t(ei[k, :, cols], a[rows, cols])
-
-            @pl.when(is_far == 0)
-            def _():
-                pu[:, uc] = v
-
-            @pl.when(is_far == 1)
-            def _():
-                pu[:, uc] = pu[:, uc] + v
+            pu[:, uc] = v + jnp.where(is_far == 1, pu[:, uc], 0.0)
 
             @pl.when(t == 0)
             def _():
@@ -500,16 +494,16 @@
     def gather(g, _):
         for o in range(8):
             t = g * 8 + o
-            gu[pl.ds(t, 1), :] = tab[pl.ds(ids[0, t], 1), :]
-            gp[pl.ds(t, 1), :] = tab[pl.ds(ids[1, t], 1), :]
-            gn[pl.ds(t, 1), :] = tab[pl.ds(ids[2, t], 1), :]
+            gu[pl.ds(t, 1), :] = tab[pl.ds(ids[t], 1), :]
+            gp[pl.ds(t, 1), :] = tab[pl.ds(ids[TB + t], 1), :]
+            gn[pl.ds(t, 1), :] = tab[pl.ds(ids[2 * TB + t], 1), :]
         return 0
 
     lax.fori_loop(0, TB // 8, gather, 0)
 
     def block(m, tot):
-        rows = pl.ds(_al(m * 128, 128), 128)
-        left = lax.broadcasted_iota(jnp.int32, (128, 128), 1) < D
+        rows = pl.ds(_al(m * 256, 256), 256)
+        left = lax.broadcasted_iota(jnp.int32, (256, 128), 1) < D
         e_u = gu[rows, :]
         e_d = gp[rows, :] - gn[rows, :]
         x = jnp.sum(jnp.where(left, e_u * e_d, 0.0), axis=1, keepdims=True)
@@ -520,7 +514,7 @@
         out[rows, :] = jnp.where(left, coef * e_d, pltpu.roll(coef * e_u, D, 1))
         return tot + jnp.sum(loss, axis=0, keepdims=True)
 
-    tot = lax.fori_loop(0, TB // 128, block, jnp.zeros((1, 1), F32))
+    tot = lax.fori_loop(0, TB // 256, block, jnp.zeros((1, 1), F32))
     out[TB:TB + 8, :] = jnp.broadcast_to(tot, (8, 128))
 
 
@@ -632,8 +626,9 @@
 
 
 def finish_kernel(*refs):
-    for src, dst in zip(refs[:4], refs[4:]):
+    for src, dst in zip(refs[:4], refs[5:9]):
         dst[...] = src[...]
+    refs[9][...] = refs[4][0:1, 0:1]
 
 
 VM = pl.BlockSpec(memory_space=pltpu.VMEM)
@@ -683,7 +678,7 @@
             out_specs=VM,
             scratch_shapes=[pltpu.VMEM((8, PR, 128), BF16), DMA((8,)), pltpu.VMEM((8 * per, 128), F32)] + [pltpu.VMEM((TB, 128), F32)] * 3,
             compiler_params=pltpu.CompilerParams(vmem_limit_bytes=VMEM_LIMIT),
-        )(table, ids)
+        )(table, ids.reshape(-1))
 
         d_u, d_i, loss = pl.pallas_call(
             backward_kernel,
@@ -701,14 +696,14 @@
             compiler_params=_params(1),
         )(a_hbm, g, cols)
         outs = (out_u, out_i, d_u, d_i)
-        out_u, out_i, d_u, d_i = pl.pallas_call(
+        out_u, out_i, d_u, d_i, loss = pl.pallas_call(
             finish_kernel,
             name='finish',
-            out_shape=tuple(jax.ShapeDtypeStruct(o.shape, o.dtype) for o in outs),
-            in_specs=[VM] * 4,
-            out_specs=(VM,) * 4,
-        )(*outs)
-        return out_u.T, out_i.T, loss[0, 0], d_u.T, d_i.T
+            out_shape=tuple(jax.ShapeDtypeStruct(o.shape, o.dtype) for o in outs) + (jax.ShapeDtypeStruct((1, 1), F32),),
+            in_specs=[VM] * 5,
+            out_specs=(VM,) * 5,
+        )(*outs, loss)
+        return out_u.T, out_i.T, loss.reshape(()), d_u.T, d_i.T
 
     user_spec = P(('row', 'col'), None)
     item_spec = P(('col', 'row'), None)

time: 237 us -> 234 us (0.987)
  Pallas kernels: 234 us -> 231 us
where the time goes in v6:
time: 234 us
  Pallas kernels  231 us (99%)
    pallas_call x1, Pallas kernels, local_fn(): pl.pallas_call(forward_kernel, name='forward', out_shape=(jax.ShapeDtypeS...  116 us
    pallas_call x1, Pallas kernels, local_fn(): pl.pallas_call(backward_kernel, name='backward', out_shape=(jax.ShapeDtyp...  104 us
    pallas_call x1, Pallas kernels, local_fn(): pl.pallas_call(lookup_kernel, name='lookup', out_shape=jax.ShapeDtypeStru...  8.44 us

profile of v6, /device:TPU:0, one launch (start us, length us, event | category | flops | bytes accessed | tf_op | source)
XLA Modules:
  0.0 233.6 jit_solution(17352954653351927547)
XLA Ops:
  0.6 0.8 fusion.2
  1.5 0.6 reshape.16.ids
  2.1 116.4 %forward.1 = (bf16[64,1024]{1,0:T(8,128)(2,1)}, bf16[64,2048]{1,0:T(8,128)(2,1)}, bf16[8,1536,128]{2,1,0:T(8,128)(2,1)}, bf16[2048,8192]{1,0:T(8,128)(2,1)}) custom-call(s32[2048,8192]{1,0:T(8,128)} %mask.1, bf16[64,1024]{1,0:T(8,128)(2,1)} %bitcast.22, bf16[64,2048]{1,0:T(8,128)(2,1)} %bitcast.20), custom_call_target="tpu_custom_call" | custom-call | tf_op jit(solution)/shard_map/forward/pallas_call | solution.py:648
  118.5 8.4 %lookup.1.g_in = f32[1032,128]{1,0:T(8,128)} custom-call(bf16[8,1536,128]{2,1,0:T(8,128)(2,1)} %get-tuple-element.20.table_hbm, s32[3072]{0:T(1024)} %reshape.16.ids), custom_call_target="tpu_custom_call" | custom-call | tf_op jit(solution)/shard_map/lookup/pallas_call | solution.py:673
  126.9 104.4 %backward.1 = (f32[64,1024]{1,0:T(8,128)}, f32[64,2048]{1,0:T(8,128)}, f32[8,128]{1,0:T(8,128)}) custom-call(bf16[2048,8192]{1,0:T(8,128)(2,1)} %get-tuple-element.19.a_hbm, f32[1032,128]{1,0:T(8,128)} %lookup.1.g_in, s32[3,8192]{1,0:T(4,128)} %bitcast.21), custom_call_target="tpu_custom_call" | custom-call | tf_op jit(solution)/shard_map/backward/pallas_call | solution.py:683
  231.3 2.3 finish.1
  (1 shorter events, 0.0 us)

commit v7 on v6

--- a/solution.py
+++ b/solution.py
@@ -454,12 +454,12 @@
             ags[s].start()
             out_i[:, s * WX:(s + 1) * WX] = t.astype(BF16)
 
-    ags = [AllGather(lk, table, PU + s * WX // 2, WX // 2, 0, iss.at[s], irs.at[s]) for s in range(SX)]
-    ag_u = AllGather(lk, table, 0, PU, 0, iss.at[SX], irs.at[SX])
+    ags = [AllGather(lk, table, PU + s * WX // 2, WX // 4, WX // 4, iss.at[s], irs.at[s]) for s in range(SX)]
+    ag_u = AllGather(lk, table, 0, PU // 2, PU // 2, iss.at[SX], irs.at[SX])
     ags.append(ag_u)
     for k in range(STEPS):
         pr.step(k, user_final, item_final, scale_near if k == 0 else None)
-    for group in ((1, 2), (3,), (0, 5, 6, 7)):
+    for group in ((1, 2), (3, 4), (0, 5, 6, 7, 8)):
         for s in (SX, 0, 1, 2, 3):
             for i in group:
                 ags[s].arrive(i)
@@ -574,10 +574,10 @@
         lax.fori_loop(0, IB // 1024, items, 0)
 
     scatter(lk.slot)
-    for group in ((0,), (1,), (2,), (5,), (6,), (3, 4), (7, 8)):
+    for group, done in (((0,), 0), ((1, 2), 1), ((), 2), ((5,), 5), ((3, 4, 6), 6), ((), 4), ((7, 8), 8)):
         for i in group:
             ag.arrive(i)
-        scatter(ag.slot(group[-1]))
+        scatter(ag.slot(done))
 
     loss = g_all[0, TB:TB + 8, :]
     for b in range(1, 8):

time: 234 us -> 230 us (0.983)
  Pallas kernels: 231 us -> 227 us
    pallas_call x1, Pallas kernels: 116 us -> 112 us  [local_fn(): pl.pallas_call(forward_kernel, name='forward', out_shape=(jax.ShapeDtypeS...]
where the time goes in v7:
time: 230 us
  Pallas kernels  227 us (99%)
    pallas_call x1, Pallas kernels, local_fn(): pl.pallas_call(forward_kernel, name='forward', out_shape=(jax.ShapeDtypeS...  112 us
    pallas_call x1, Pallas kernels, local_fn(): pl.pallas_call(backward_kernel, name='backward', out_shape=(jax.ShapeDtyp...  105 us
    pallas_call x1, Pallas kernels, local_fn(): pl.pallas_call(lookup_kernel, name='lookup', out_shape=jax.ShapeDtypeStru...  8.44 us

profile of v7, /device:TPU:0, one launch (start us, length us, event | category | flops | bytes accessed | tf_op | source)
XLA Modules:
  0.0 229.5 jit_solution(5623942553313805490)
XLA Ops:
  0.6 0.8 fusion.2
  1.5 0.6 reshape.16.ids
  2.1 112.2 %forward.1 = (bf16[64,1024]{1,0:T(8,128)(2,1)}, bf16[64,2048]{1,0:T(8,128)(2,1)}, bf16[8,1536,128]{2,1,0:T(8,128)(2,1)}, bf16[2048,8192]{1,0:T(8,128)(2,1)}) custom-call(s32[2048,8192]{1,0:T(8,128)} %mask.1, bf16[64,1024]{1,0:T(8,128)(2,1)} %bitcast.22, bf16[64,2048]{1,0:T(8,128)(2,1)} %bitcast.20), custom_call_target="tpu_custom_call" | custom-call | tf_op jit(solution)/shard_map/forward/pallas_call | solution.py:648
  114.3 8.4 %lookup.1.g_in = f32[1032,128]{1,0:T(8,128)} custom-call(bf16[8,1536,128]{2,1,0:T(8,128)(2,1)} %get-tuple-element.20.table_hbm, s32[3072]{0:T(1024)} %reshape.16.ids), custom_call_target="tpu_custom_call" | custom-call | tf_op jit(solution)/shard_map/lookup/pallas_call | solution.py:673
  122.7 104.5 %backward.1 = (f32[64,1024]{1,0:T(8,128)}, f32[64,2048]{1,0:T(8,128)}, f32[8,128]{1,0:T(8,128)}) custom-call(bf16[2048,8192]{1,0:T(8,128)(2,1)} %get-tuple-element.19.a_hbm, f32[1032,128]{1,0:T(8,128)} %lookup.1.g_in, s32[3,8192]{1,0:T(4,128)} %bitcast.21), custom_call_target="tpu_custom_call" | custom-call | tf_op jit(solution)/shard_map/backward/pallas_call | solution.py:683
  227.3 2.3 finish.1
  (1 shorter events, 0.0 us)

commit v8 on v7

--- a/solution.py
+++ b/solution.py
@@ -492,14 +492,14 @@
     lax.fori_loop(0, 8, unpack, 0)
 
     def gather(g, _):
-        for o in range(8):
-            t = g * 8 + o
+        for o in range(16):
+            t = g * 16 + o
             gu[pl.ds(t, 1), :] = tab[pl.ds(ids[t], 1), :]
             gp[pl.ds(t, 1), :] = tab[pl.ds(ids[TB + t], 1), :]
             gn[pl.ds(t, 1), :] = tab[pl.ds(ids[2 * TB + t], 1), :]
         return 0
 
-    lax.fori_loop(0, TB // 8, gather, 0)
+    lax.fori_loop(0, TB // 16, gather, 0)
 
     def block(m, tot):
         rows = pl.ds(_al(m * 256, 256), 256)
@@ -591,6 +591,11 @@
         left = lax.broadcasted_iota(jnp.int32, (n, 128), 1) < D
         return jnp.where(left, s[:n], pltpu.roll(s[n:], D, 1)).T
 
+    xu = seed(acc_u[...])
+    for s in range(SY):
+        v = xu[:D] if s == 0 else xu[D:]
+        su[:, s * WY:(s + 1) * WY] = v
+        pr.put_user(0, s, v.astype(BF16))
     xi = seed(acc_i[...])
     for s in range(SX):
         src = xi[:D] if s < SX // 2 else xi[D:]
@@ -598,11 +603,6 @@
         v = src[:, o:o + WX]
         si[:, s * WX:(s + 1) * WX] = v
         pr.put_item(0, s, v.astype(BF16))
-    xu = seed(acc_u[...])
-    for s in range(SY):
-        v = xu[:D] if s == 0 else xu[D:]
-        su[:, s * WY:(s + 1) * WY] = v
-        pr.put_user(0, s, v.astype(BF16))
 
     def user_final(k, s, v):
         v = su[:, s * WY:(s + 1) * WY] + v

time: 230 us -> 229 us (level)
  no operation moved by 1% of the time
where the time goes in v8:
time: 229 us
  Pallas kernels  226 us (99%)
    pallas_call x1, Pallas kernels, local_fn(): pl.pallas_call(forward_kernel, name='forward', out_shape=(jax.ShapeDtypeS...  112 us
    pallas_call x1, Pallas kernels, local_fn(): pl.pallas_call(backward_kernel, name='backward', out_shape=(jax.ShapeDtyp...  104 us
    pallas_call x1, Pallas kernels, local_fn(): pl.pallas_call(lookup_kernel, name='lookup', out_shape=jax.ShapeDtypeStru...  8.1 us

profile of v8, /device:TPU:0, one launch (start us, length us, event | category | flops | bytes accessed | tf_op | source)
XLA Modules:
  0.0 228.6 jit_solution(16628756474072353827)
XLA Ops:
  0.6 0.8 fusion.2
  1.5 0.6 reshape.16.ids
  2.1 112.2 %forward.1 = (bf16[64,1024]{1,0:T(8,128)(2,1)}, bf16[64,2048]{1,0:T(8,128)(2,1)}, bf16[8,1536,128]{2,1,0:T(8,128)(2,1)}, bf16[2048,8192]{1,0:T(8,128)(2,1)}) custom-call(s32[2048,8192]{1,0:T(8,128)} %mask.1, bf16[64,1024]{1,0:T(8,128)(2,1)} %bitcast.22, bf16[64,2048]{1,0:T(8,128)(2,1)} %bitcast.20), custom_call_target="tpu_custom_call" | custom-call | tf_op jit(solution)/shard_map/forward/pallas_call | solution.py:648
  114.3 8.1 %lookup.1.g_in = f32[1032,128]{1,0:T(8,128)} custom-call(bf16[8,1536,128]{2,1,0:T(8,128)(2,1)} %get-tuple-element.20.table_hbm, s32[3072]{0:T(1024)} %reshape.16.ids), custom_call_target="tpu_custom_call" | custom-call | tf_op jit(solution)/shard_map/lookup/pallas_call | solution.py:673
  122.4 103.9 %backward.1 = (f32[64,1024]{1,0:T(8,128)}, f32[64,2048]{1,0:T(8,128)}, f32[8,128]{1,0:T(8,128)}) custom-call(bf16[2048,8192]{1,0:T(8,128)(2,1)} %get-tuple-element.19.a_hbm, f32[1032,128]{1,0:T(8,128)} %lookup.1.g_in, s32[3,8192]{1,0:T(4,128)} %bitcast.21), custom_call_target="tpu_custom_call" | custom-call | tf_op jit(solution)/shard_map/backward/pallas_call | solution.py:683
  226.3 2.3 finish.1
  (1 shorter events, 0.0 us)
